TPU v7x, 32 devices: a 4x2x2 block of a 4x4x8 slice. The times are simulated.
32 devices in a mesh: data: 4 (over y, z), tp: 8 (over x, core).
Axes of the slice: x: 4, y: 2, z: 2, core: 2. Of those that a mesh axis runs over, the one named last changes fastest.
The devices are a block of a 4x4x8 slice.
Arguments:
- attn_out: bfloat16 [1024, 16384], P('data', 'tp'), parts along dimension 0
- w_out: bfloat16 [16384, 16384], P('tp')
- residual: bfloat16 [1024, 16384], P('data', 'tp'), parts along dimension 0
- norm_gain: float32 [16384], P('tp')
Outputs:
- output 1: bfloat16 [1024, 16384], P('data', 'tp'), parts along dimension 0
- output 2: bfloat16 [1024, 16384], P('data', 'tp'), parts along dimension 0
There are 4 independent parts. A program takes and returns all parts, laid end to end along the dimension named above; an argument that names none is the same for every part.
All inputs are finite; a program needn't handle non-finite values.
Results may differ from a plain program's by a relative error of at most 0.00634236.
Values are sent between devices in bfloat16 or wider.
A program may use at most 768 MiB of HBM per device.

v0:
```python
import jax
import jax.numpy as jnp
from jax import lax
from jax.sharding import PartitionSpec as P, NamedSharding

EPS = 1e-5


def solution(mesh):
    tp_size = mesh.shape["tp"]

    def local_step(attn_blk, w_blk, resid_blk, gain_blk):
        tok_rows = attn_blk.shape[0]
        d_local = resid_blk.shape[1]
        d_model = d_local * tp_size
        partial = jnp.dot(attn_blk, w_blk, preferred_element_type=jnp.float32).astype(jnp.bfloat16)
        received = lax.all_to_all(partial, "tp", 1, 0, tiled=True)
        projected = jnp.sum(received.reshape(tp_size, tok_rows, d_local), axis=0, dtype=jnp.float32)
        hidden = resid_blk.astype(jnp.float32) + projected
        sq_part = jnp.sum(hidden * hidden, axis=-1, keepdims=True)
        sq_total = lax.psum(sq_part, "tp")
        normed = hidden * lax.rsqrt(sq_total / d_model + EPS) * gain_blk
        return hidden.astype(jnp.bfloat16), normed.astype(jnp.bfloat16)

    return jax.shard_map(
        local_step,
        mesh=mesh,
        in_specs=(P("data", "tp"), P("tp", None), P("data", "tp"), P("tp")),
        out_specs=(P("data", "tp"), P("data", "tp")),
        check_vma=False,
    )
```

profile of v0, /device:TPU:81, one launch (start us, length us, event | category | flops | bytes accessed | tf_op | source)
XLA Modules:
  0.0 157.6 jit_solution(16447513905032473990)
XLA Ops:
  0.6 0.0 copy-start
  0.6 1.2 copy-done
  1.9 30.1 %convolution_convert_fusion = bf16[256,16384]{1,0:T(8,128)(2,1)} fusion(bf16[256,2048]{1,0:T(8,128)(2,1)S(1)} %copy-done, bf16[2048,16384]{1,0:T(8,128)(2,1)} %param.5), kind=kOutput, calls=%fused_computation | convolution fusion | flops 17184063488 | bytes 76546048 | tf_op jit(solution)/shard_map/dot_general | solution.py:16
  31.9 8.3 %copy.9 = bf16[32,8,8,2048]{3,2,0,1:T(8,128)(2,1)} copy(bf16[32,8,8,2048]{3,2,1,0:T(8,128)(2,1)} %bitcast.9) | data formatting | bytes 16777216 | tf_op jit(solution)/shard_map/all_to_all | solution.py:17
  40.2 99.4 %all_to_all.13 = bf16[256,8,2048]{2,0,1:T(8,128)(2,1)S(1)} all-to-all(bf16[256,8,2048]{2,0,1:T(8,128)(2,1)} %bitcast.8), channel_id=1, replica_groups=mesh['data'=4,'tp'=8] {'tp'}, dimensions={1} | all-to-all | bytes 16777216 | tf_op jit(solution)/shard_map/all_to_all | solution.py:17
  139.6 0.0 copy-start.1
  139.6 1.8 %convert_reduce_fusion = f32[256,2048]{1,0:T(8,128)S(1)} fusion(bf16[256,8,2048]{2,0,1:T(8,128)(2,1)S(1)} %all_to_all.13), kind=kLoop, calls=%fused_computation.1 | loop fusion | flops 7864320 | bytes 10485760 | tf_op jit(solution)/shard_map/reduce_sum | solution.py:18
  141.4 0.0 copy-done.1
  141.4 0.0 copy-start.2
  141.4 0.4 multiply_reduce_fusion
  141.8 12.9 %psum.7 = f32[256,1]{0,1:T(1,128)S(1)} all-reduce(f32[256,1]{0,1:T(1,128)S(1)} %bitcast.10), channel_id=1, replica_groups=mesh['data'=4,'tp'=8] {'tp'}, use_global_device_ids=true, to_apply=%region_2.0 | all-reduce | flops 256 | bytes 2048 | tf_op jit(solution)/shard_map/psum | solution.py:21
  154.7 0.0 copy-done.2
  154.7 2.9 %multiply_convert_fusion = (bf16[256,2048]{1,0:T(8,128)(2,1)}, bf16[256,2048]{1,0:T(8,128)(2,1)}) fusion(f32[2048]{0:T(1024)S(1)} %copy-done.2, f32[256]{0:T(256)S(1)} %bitcast.11, f32[256,2048]{1,0:T(8,128)S(1)} %convert_reduce_fusion, bf16[256,2048]{1,0:T(8,128)(2,1)} %param.6), kind=kLoop, calls=%fused_computation.3 | loop fusion | flops 3145728 | bytes 5252096 | tf_op jit(solution)/shard_map/convert_element_type | solution.py:23
  (1 shorter events, 0.0 us)
Async XLA Ops:
  0.6 1.2 copy-start
  139.6 1.8 %copy-start.1 = (bf16[256,2048]{1,0:T(8,128)(2,1)S(1)}, bf16[256,2048]{1,0:T(8,128)(2,1)}, u32[]{:S(2)}) copy-start(bf16[256,2048]{1,0:T(8,128)(2,1)} %param.6) | copy-start | bytes 3145732
  141.4 13.3 %copy-start.2 = (f32[2048]{0:T(1024)S(1)}, f32[2048]{0:T(1024)}, u32[]{:S(2)}) copy-start(f32[2048]{0:T(1024)} %param.7) | copy-start | bytes 24580
where the time goes:
time: 158 us
  blocking collectives  112 us (71%)
  matrix products  30.1 us (19%)
  local copies, waits for them, and re-layouts  9.49 us (6%)
  other arithmetic  5.06 us (3%)
    all_to_all x1, blocking collectives, local_step(): received = lax.all_to_all(partial, 'tp', 1, 0, tiled=True)  99.4 us
    dot_general x1, matrix products, local_step(): jnp.dot(attn_blk, w_blk, preferred_element_type=jnp.float32)  30.1 us
    psum x1, blocking collectives, local_step(): sq_total = lax.psum(sq_part, 'tp')  12.9 us
    all_to_all x1, local copies, waits for them, and re-layouts, local_step(): received = lax.all_to_all(partial, 'tp', 1, 0, tiled=True)  8.25 us

commit v1 on v0

v1 whole, which is shorter than its diff:
```python
import functools

import jax
import jax.numpy as jnp
from jax import lax
from jax.experimental import pallas as pl
from jax.experimental.pallas import tpu as pltpu
from jax.sharding import PartitionSpec as P

EPS = 1e-5
CORES = 2
COLS = 512
W_SLOTS = 3


def kernel(
    tp, tok_rows, d_local, a_hbm, w_hbm, r_hbm, g_ref, hid_hbm, nrm_hbm,
    a, w, part, recv, relay_out, relay_in, res, hid, hid_bf, nrm_bf, sq_lanes, sq_all,
    a_sem, w_sem, r_sem, send_sem, recv_sem, rsend_sem, rrecv_sem, qsend_sem, qrecv_sem,
    out_sem,
):
    chips = tp // CORES
    half = d_local // 2
    pp = half // COLS
    blk = 4 * pp
    me = lax.axis_index("tp")
    chip, core = me // CORES, me % CORES

    def w_col(g):
        b, i = g % 2, (g % blk) // 2
        s, p, ph = i % 2, i // 2, g // blk
        is0 = (3 - ph) * (2 - ph) * (1 - ph) // 6
        is1 = ph * (3 - ph) * (2 - ph) // 2
        is2 = ph * (3 - ph) * (ph - 1) // 2
        kept = ph // 2
        step = 2 * s - 1
        hop = is0 * 2 + is1 * step + kept * (1 - b) * step
        to_core = (1 - kept) * b + is2 * (1 - core) + (kept - is2) * core
        in_half = s + is1 * (1 - 2 * s)
        to = ((chip + chips + hop) % chips) * CORES + to_core
        return to * d_local + in_half * half + p * COLS

    def w_copy(g):
        slot = g % W_SLOTS
        cols = pl.ds(pl.multiple_of(w_col(g), COLS), COLS)
        return pltpu.make_async_copy(w_hbm.at[:, cols], w.at[slot], w_sem.at[slot])

    def piece_copy(g):
        b, i = g % 2, (g % blk) // 2
        s, ph = i % 2, g // blk
        far = 1 - ph // 2
        to_chip = (chip + chips + far * (2 * s - 1)) % chips
        to_core = far * b + (1 - far) * (1 - core)
        slot = g + far * (core - b)
        return pltpu.make_async_remote_copy(
            src_ref=part.at[g],
            dst_ref=recv.at[slot],
            send_sem=send_sem.at[g],
            recv_sem=recv_sem.at[slot],
            device_id={"tp": to_chip * CORES + to_core},
            device_id_type=pl.DeviceIdType.MESH,
        )

    def recv_wait(slot):
        pltpu.make_async_copy(recv.at[slot], recv.at[slot], recv_sem.at[slot]).wait()

    def relay_copy(i):
        to_chip = (chip + chips + 2 * (i % 2) - 1) % chips
        return pltpu.make_async_remote_copy(
            src_ref=relay_out.at[i],
            dst_ref=relay_in.at[i],
            send_sem=rsend_sem.at[i],
            recv_sem=rrecv_sem.at[i],
            device_id={"tp": to_chip * CORES + core},
            device_id_type=pl.DeviceIdType.MESH,
        )

    def sq_copy(j):
        return pltpu.make_async_remote_copy(
            src_ref=sq_all.at[me],
            dst_ref=sq_all.at[me],
            send_sem=qsend_sem.at[j],
            recv_sem=qrecv_sem.at[me],
            device_id={"tp": (me + j) % tp},
            device_id_type=pl.DeviceIdType.MESH,
        )

    a_copy = pltpu.make_async_copy(a_hbm, a, a_sem)
    r_copy = pltpu.make_async_copy(r_hbm, res, r_sem)
    a_copy.start()
    for g in range(W_SLOTS):
        w_copy(g).start()
    barrier = pltpu.get_barrier_semaphore()
    for j in range(1, tp):
        pl.semaphore_signal(
            barrier, inc=1, device_id={"tp": (me + j) % tp}, device_id_type=pl.DeviceIdType.MESH
        )
    pl.semaphore_wait(barrier, tp - 1)
    a_copy.wait()

    def project(g, carry):
        slot = g % W_SLOTS
        w_copy(g).wait()
        part[g] = jnp.dot(a[...], w[slot], preferred_element_type=jnp.float32).astype(jnp.bfloat16)

        @pl.when(g < 3 * blk)
        def _():
            piece_copy(g).start()

        @pl.when(g + W_SLOTS < 4 * blk)
        def _():
            w_copy(g + W_SLOTS).start()

        return carry

    lax.fori_loop(0, 4 * blk, project, 0)
    r_copy.start()

    def relay(i, carry):
        recv_wait(2 * i)
        recv_wait(2 * i + 1)
        recv_wait(2 * blk + 2 * i)
        relay_out[i] = (
            recv[2 * i].astype(jnp.float32)
            + recv[2 * i + 1].astype(jnp.float32)
            + recv[2 * blk + 2 * i].astype(jnp.float32)
            + part[3 * blk + 2 * i].astype(jnp.float32)
        )
        relay_copy(i).start()
        return carry

    lax.fori_loop(0, 2 * pp, relay, 0)
    r_copy.wait()

    def columns(i):
        return pl.ds(pl.multiple_of((i % 2) * half + (i // 2) * COLS, COLS), COLS)

    def gather(i, carry):
        direct = blk + 2 * (i + 1 - 2 * (i % 2))
        recv_wait(direct)
        recv_wait(direct + 1)
        recv_wait(2 * blk + 2 * i + 1)
        hid[i] = (
            res[:, columns(i)].astype(jnp.float32)
            + part[3 * blk + 2 * i + 1].astype(jnp.float32)
            + recv[2 * blk + 2 * i + 1].astype(jnp.float32)
            + recv[direct].astype(jnp.float32)
            + recv[direct + 1].astype(jnp.float32)
        )
        return carry

    lax.fori_loop(0, 2 * pp, gather, 0)
    sq_lanes[...] = jnp.zeros_like(sq_lanes)

    def hid_out(i):
        return pltpu.make_async_copy(
            hid_bf.at[:, columns(i)], hid_hbm.at[:, columns(i)], out_sem.at[i]
        )

    def nrm_out(i):
        return pltpu.make_async_copy(
            nrm_bf.at[:, columns(i)], nrm_hbm.at[:, columns(i)], out_sem.at[2 * pp + i]
        )

    def finish(i, carry):
        relay_copy(i).wait_recv()
        h = hid[i] + relay_in[i]
        hid[i] = h
        hid_bf[:, columns(i)] = h.astype(jnp.bfloat16)
        hid_out(i).start()
        sq = h * h
        total = sq_lanes[...]
        for c in range(COLS // 128):
            total += sq[:, c * 128 : (c + 1) * 128]
        sq_lanes[...] = total
        return carry

    lax.fori_loop(0, 2 * pp, finish, 0)

    by_lane = jnp.transpose(sq_lanes[...])
    sq_all[me] = jnp.sum(by_lane.reshape(16, 8, tok_rows), axis=0)
    for j in range(1, tp):
        sq_copy(j).start()
    for j in range(1, tp):
        peer = (me + j) % tp
        pltpu.make_async_copy(sq_all.at[peer], sq_all.at[peer], qrecv_sem.at[peer]).wait()
    sq_total = jnp.sum(jnp.sum(sq_all[...], axis=0), axis=0, keepdims=True)
    scale_row = lax.rsqrt(sq_total / (d_local * tp) + EPS)
    scale = jnp.transpose(jnp.broadcast_to(scale_row, (128, tok_rows)))

    def normalize(i, carry):
        for c in range(COLS // 128):
            lanes = pl.ds(pl.multiple_of((i % 2) * half + (i // 2) * COLS + c * 128, 128), 128)
            normed = hid[i, :, c * 128 : (c + 1) * 128] * scale * g_ref[:, lanes]
            nrm_bf[:, lanes] = normed.astype(jnp.bfloat16)
        nrm_out(i).start()
        return carry

    lax.fori_loop(0, 2 * pp, normalize, 0)

    def drain(g, carry):
        piece_copy(g).wait_send()
        return carry

    lax.fori_loop(0, 3 * blk, drain, 0)
    for i in range(2 * pp):
        relay_copy(i).wait_send()
        hid_out(i).wait()
        nrm_out(i).wait()
    for j in range(1, tp):
        sq_copy(j).wait_send()


def solution(mesh):
    tp = mesh.shape["tp"]

    def local_step(attn_blk, w_blk, resid_blk, gain_blk):
        tok_rows, depth = attn_blk.shape
        d_local = resid_blk.shape[1]
        pp = d_local // 2 // COLS
        f32, bf16 = jnp.float32, jnp.bfloat16
        piece = (tok_rows, COLS)
        dma = pltpu.SemaphoreType.DMA
        anywhere = pl.BlockSpec(memory_space=pl.ANY)
        return pl.pallas_call(
            functools.partial(kernel, tp, tok_rows, d_local),
            out_shape=[jax.ShapeDtypeStruct((tok_rows, d_local), bf16)] * 2,
            in_specs=[anywhere] * 3 + [pl.BlockSpec(memory_space=pltpu.VMEM)],
            out_specs=[anywhere] * 2,
            scratch_shapes=[
                pltpu.VMEM((tok_rows, depth), bf16),
                pltpu.VMEM((W_SLOTS, depth, COLS), bf16),
                pltpu.VMEM((16 * pp, *piece), bf16),
                pltpu.VMEM((12 * pp, *piece), bf16),
                pltpu.VMEM((2 * pp, *piece), f32),
                pltpu.VMEM((2 * pp, *piece), f32),
                pltpu.VMEM((tok_rows, d_local), bf16),
                pltpu.VMEM((2 * pp, *piece), f32),
                pltpu.VMEM((tok_rows, d_local), bf16),
                pltpu.VMEM((tok_rows, d_local), bf16),
                pltpu.VMEM((tok_rows, 128), f32),
                pltpu.VMEM((tp, 8, tok_rows), f32),
                dma,
                dma((W_SLOTS,)),
                dma,
                dma((12 * pp,)),
                dma((12 * pp,)),
                dma((2 * pp,)),
                dma((2 * pp,)),
                dma((tp,)),
                dma((tp,)),
                dma((4 * pp,)),
            ],
            compiler_params=pltpu.CompilerParams(
                collective_id=0, has_side_effects=True, vmem_limit_bytes=60 * 2**20
            ),
            name="project_reduce_norm",
        )(attn_blk, w_blk, resid_blk, gain_blk.reshape(1, d_local))

    return jax.shard_map(
        local_step,
        mesh=mesh,
        in_specs=(P("data", "tp"), P("tp", None), P("data", "tp"), P("tp")),
        out_specs=(P("data", "tp"), P("data", "tp")),
        check_vma=False,
    )
```

time: 158 us -> 88.1 us (0.56)
  blocking collectives: 112 us -> 0 us
  Pallas kernels: 0 us -> 82.6 us
  matrix products: 30.1 us -> 0 us
  other arithmetic: 5.06 us -> 0 us
  local copies, waits for them, and re-layouts: 9.49 us -> 4.61 us
    all_to_all x1 -> x0, blocking collectives: 99.4 us -> none  [local_step(): received = lax.all_to_all(partial, 'tp', 1, 0, tiled=True)]
    pallas_call x0 -> x1, Pallas kernels: none -> 82.6 us  [local_step(): pl.pallas_call(functools.partial(kernel, tp, tok_rows, d_local), out_shap...]
    dot_general x1 -> x0, matrix products: 30.1 us -> none  [local_step(): jnp.dot(attn_blk, w_blk, preferred_element_type=jnp.float32)]
    psum x1 -> x0, blocking collectives: 12.9 us -> none  [local_step(): sq_total = lax.psum(sq_part, 'tp')]
    all_to_all x1 -> x0, local copies, waits for them, and re-layouts: 8.25 us -> none  [local_step(): received = lax.all_to_all(partial, 'tp', 1, 0, tiled=True)]
    unnamed x6 -> x2, local copies, waits for them, and re-layouts: 1.23 us -> 4.61 us
    convert_element_type x1 -> x0, other arithmetic: 2.89 us -> none  [local_step(): return (hidden.astype(jnp.bfloat16), normed.astype(jnp.bfloat16))]
    reduce_sum x2 -> x0, other arithmetic: 2.16 us -> none  [the longest x1 1.78 us: local_step(): jnp.sum(received.reshape(tp_size, tok_rows, d_local), axis=0, dtype=jnp.f...]
where the time goes in v1:
time: 88.1 us; the launch traced here: 87.9 us
  Pallas kernels  82.6 us (94%)
  local copies, waits for them, and re-layouts  4.61 us (5%)
    pallas_call x1, Pallas kernels, local_step(): pl.pallas_call(functools.partial(kernel, tp, tok_rows, d_local), out_shap...  82.6 us
    unnamed x2, local copies, waits for them, and re-layouts  4.61 us

profile of v1, /device:TPU:81, one launch (start us, length us, event | category | flops | bytes accessed | tf_op | source)
XLA Modules:
  0.0 87.9 jit_solution(17308935006929192211)
XLA Ops:
  0.6 82.6 %project_reduce_norm.1 = (bf16[256,2048]{1,0:T(8,128)(2,1)}, bf16[256,2048]{1,0:T(8,128)(2,1)}) custom-call(bf16[256,2048]{1,0:T(8,128)(2,1)} %a_hbm.1, bf16[2048,16384]{1,0:T(8,128)(2,1)} %w_hbm.1, bf16[256,2048]{1,0:T(8,128)(2,1)} %r_hbm.1, f32[1,2048]{1,0:T(1,128)} %bitcast.1), custom_call_target="tpu_custom_call" | custom-call | tf_op jit(solution)/shard_map/project_reduce_norm/pallas_call | solution.py:225
  83.3 2.3 %copy.8 = bf16[256,2048]{1,0:T(8,128)(2,1)} copy(bf16[256,2048]{1,0:T(8,128)(2,1)} %get-tuple-element.4) | data formatting | bytes 2097152
  85.6 2.3 %copy.9 = bf16[256,2048]{1,0:T(8,128)(2,1)} copy(bf16[256,2048]{1,0:T(8,128)(2,1)} %get-tuple-element.5) | data formatting | bytes 2097152

commit v2 on v1

v2 whole, which is shorter than its diff:
```python
import functools

import jax
import jax.numpy as jnp
from jax import lax
from jax.experimental import pallas as pl
from jax.experimental.pallas import tpu as pltpu
from jax.sharding import PartitionSpec as P

EPS = 1e-5
CORES = 2
COLS = 512
W_SLOTS = 3
ROWS = 128


def kernel(
    tp, tok_rows, d_local, a_hbm, w_hbm, r_hbm, g_ref, hid_out, nrm_out,
    a, w, part, recv, relay_out, relay_in, res, hid, sq_all,
    a_sem, w_sem, r_sem, send_sem, recv_sem, rsend_sem, rrecv_sem, qsend_sem, qrecv_sem,
):
    chips = tp // CORES
    half = d_local // 2
    pp = half // COLS
    blk = 4 * pp
    me = lax.axis_index("tp")
    chip, core = me // CORES, me % CORES

    def w_col(g):
        b, i = g % 2, (g % blk) // 2
        s, p, ph = i % 2, i // 2, g // blk
        is0 = (3 - ph) * (2 - ph) * (1 - ph) // 6
        is1 = ph * (3 - ph) * (2 - ph) // 2
        is2 = ph * (3 - ph) * (ph - 1) // 2
        kept = ph // 2
        step = 2 * s - 1
        hop = is0 * 2 + is1 * step + kept * (1 - b) * step
        to_core = (1 - kept) * b + is2 * (1 - core) + (kept - is2) * core
        in_half = s + is1 * (1 - 2 * s)
        to = ((chip + chips + hop) % chips) * CORES + to_core
        return to * d_local + in_half * half + p * COLS

    def w_copy(g):
        slot = g % W_SLOTS
        cols = pl.ds(pl.multiple_of(w_col(g), COLS), COLS)
        return pltpu.make_async_copy(w_hbm.at[:, cols], w.at[slot], w_sem.at[slot])

    def piece_copy(g):
        b, i = g % 2, (g % blk) // 2
        s, ph = i % 2, g // blk
        far = 1 - ph // 2
        to_chip = (chip + chips + far * (2 * s - 1)) % chips
        to_core = far * b + (1 - far) * (1 - core)
        slot = g + far * (core - b)
        return pltpu.make_async_remote_copy(
            src_ref=part.at[g],
            dst_ref=recv.at[slot],
            send_sem=send_sem.at[g],
            recv_sem=recv_sem.at[slot],
            device_id={"tp": to_chip * CORES + to_core},
            device_id_type=pl.DeviceIdType.MESH,
        )

    def recv_wait(slot):
        pltpu.make_async_copy(recv.at[slot], recv.at[slot], recv_sem.at[slot]).wait()

    def relay_copy(i):
        to_chip = (chip + chips + 2 * (i % 2) - 1) % chips
        return pltpu.make_async_remote_copy(
            src_ref=relay_out.at[i],
            dst_ref=relay_in.at[i],
            send_sem=rsend_sem.at[i],
            recv_sem=rrecv_sem.at[i],
            device_id={"tp": to_chip * CORES + core},
            device_id_type=pl.DeviceIdType.MESH,
        )

    def sq_copy(rb, j):
        return pltpu.make_async_remote_copy(
            src_ref=sq_all.at[rb, me],
            dst_ref=sq_all.at[rb, me],
            send_sem=qsend_sem.at[rb, j],
            recv_sem=qrecv_sem.at[rb, me],
            device_id={"tp": (me + j) % tp},
            device_id_type=pl.DeviceIdType.MESH,
        )

    a_copy = pltpu.make_async_copy(a_hbm, a, a_sem)
    r_copy = pltpu.make_async_copy(r_hbm, res, r_sem)
    a_copy.start()
    for g in range(W_SLOTS):
        w_copy(g).start()
    barrier = pltpu.get_barrier_semaphore()
    for j in range(1, tp):
        pl.semaphore_signal(
            barrier, inc=1, device_id={"tp": (me + j) % tp}, device_id_type=pl.DeviceIdType.MESH
        )
    pl.semaphore_wait(barrier, tp - 1)
    a_copy.wait()

    def project(g, carry):
        slot = g % W_SLOTS
        w_copy(g).wait()
        part[g] = jnp.dot(a[...], w[slot], preferred_element_type=jnp.float32).astype(jnp.bfloat16)

        @pl.when(g < 3 * blk)
        def _():
            piece_copy(g).start()

        @pl.when(g + W_SLOTS < 4 * blk)
        def _():
            w_copy(g + W_SLOTS).start()

        return carry

    lax.fori_loop(0, 4 * blk, project, 0)
    r_copy.start()

    def row_block(rb):
        return pl.ds(pl.multiple_of(rb * ROWS, ROWS), ROWS)

    for i in range(2 * pp):
        recv_wait(2 * i)
        recv_wait(2 * i + 1)
        recv_wait(2 * blk + 2 * i)

    def relay(j, carry):
        rows, s = row_block(j // 2), j % 2
        for p in range(pp):
            i = 2 * p + s
            relay_out[j, :, p * COLS : (p + 1) * COLS] = (
                recv[2 * i, rows].astype(jnp.float32)
                + recv[2 * i + 1, rows].astype(jnp.float32)
                + recv[2 * blk + 2 * i, rows].astype(jnp.float32)
                + part[3 * blk + 2 * i, rows].astype(jnp.float32)
            )
        relay_copy(j).start()
        return carry

    lax.fori_loop(0, 2 * (tok_rows // ROWS), relay, 0)
    r_copy.wait()

    def gather(i, carry):
        cols = pl.ds(pl.multiple_of((i % 2) * half + (i // 2) * COLS, COLS), COLS)
        direct = blk + 2 * (i + 1 - 2 * (i % 2))
        recv_wait(direct)
        recv_wait(direct + 1)
        recv_wait(2 * blk + 2 * i + 1)
        hid[:, cols] = (
            res[:, cols].astype(jnp.float32)
            + part[3 * blk + 2 * i + 1].astype(jnp.float32)
            + recv[2 * blk + 2 * i + 1].astype(jnp.float32)
            + recv[direct].astype(jnp.float32)
            + recv[direct + 1].astype(jnp.float32)
        )
        return carry

    lax.fori_loop(0, 2 * pp, gather, 0)

    def finish(rb, carry):
        rows = row_block(rb)
        total = jnp.zeros((ROWS, 128), jnp.float32)
        for s in range(2):
            relay_copy(2 * rb + s).wait_recv()
            for c in range(0, half, 128):
                cols = slice(s * half + c, s * half + c + 128)
                h = hid[rows, cols] + relay_in[2 * rb + s, :, c : c + 128]
                hid[rows, cols] = h
                hid_out[rows, cols] = h.astype(jnp.bfloat16)
                total += h * h
        sq_all[rb, me] = jnp.sum(jnp.transpose(total).reshape(16, 8, ROWS), axis=0)
        for j in range(1, tp):
            sq_copy(rb, j).start()
        for j in range(1, tp):
            peer = (me + j) % tp
            pltpu.make_async_copy(
                sq_all.at[rb, peer], sq_all.at[rb, peer], qrecv_sem.at[rb, peer]
            ).wait()
        sq_total = jnp.sum(jnp.sum(sq_all[rb], axis=0), axis=0, keepdims=True)
        scale_row = lax.rsqrt(sq_total / (d_local * tp) + EPS)
        scale = jnp.transpose(jnp.broadcast_to(scale_row, (128, ROWS)))
        for c in range(0, d_local, 128):
            normed = hid[rows, c : c + 128] * scale * g_ref[:, c : c + 128]
            nrm_out[rows, c : c + 128] = normed.astype(jnp.bfloat16)
        return carry

    lax.fori_loop(0, tok_rows // ROWS, finish, 0)

    def drain(g, carry):
        piece_copy(g).wait_send()
        return carry

    lax.fori_loop(0, 3 * blk, drain, 0)
    for j in range(2 * (tok_rows // ROWS)):
        relay_copy(j).wait_send()
    for rb in range(tok_rows // ROWS):
        for j in range(1, tp):
            sq_copy(rb, j).wait_send()


def solution(mesh):
    tp = mesh.shape["tp"]

    def local_step(attn_blk, w_blk, resid_blk, gain_blk):
        tok_rows, depth = attn_blk.shape
        d_local = resid_blk.shape[1]
        pp = d_local // 2 // COLS
        blocks = tok_rows // ROWS
        f32, bf16 = jnp.float32, jnp.bfloat16
        piece = (tok_rows, COLS)
        dma = pltpu.SemaphoreType.DMA
        anywhere = pl.BlockSpec(memory_space=pl.ANY)
        return pl.pallas_call(
            functools.partial(kernel, tp, tok_rows, d_local),
            out_shape=[pltpu.VMEM((tok_rows, d_local), bf16)] * 2,
            in_specs=[anywhere] * 3 + [pl.BlockSpec(memory_space=pltpu.VMEM)],
            out_specs=[pl.BlockSpec(memory_space=pltpu.VMEM)] * 2,
            scratch_shapes=[
                pltpu.VMEM((tok_rows, depth), bf16),
                pltpu.VMEM((W_SLOTS, depth, COLS), bf16),
                pltpu.VMEM((16 * pp, *piece), bf16),
                pltpu.VMEM((12 * pp, *piece), bf16),
                pltpu.VMEM((2 * blocks, ROWS, d_local // 2), f32),
                pltpu.VMEM((2 * blocks, ROWS, d_local // 2), f32),
                pltpu.VMEM((tok_rows, d_local), bf16),
                pltpu.VMEM((tok_rows, d_local), f32),
                pltpu.VMEM((blocks, tp, 8, ROWS), f32),
                dma,
                dma((W_SLOTS,)),
                dma,
                dma((12 * pp,)),
                dma((12 * pp,)),
                dma((2 * blocks,)),
                dma((2 * blocks,)),
                dma((blocks, tp)),
                dma((blocks, tp)),
            ],
            compiler_params=pltpu.CompilerParams(
                collective_id=0, has_side_effects=True, vmem_limit_bytes=56 * 2**20
            ),
            name="project_reduce_norm",
        )(attn_blk, w_blk, resid_blk, gain_blk.reshape(1, d_local))

    return jax.shard_map(
        local_step,
        mesh=mesh,
        in_specs=(P("data", "tp"), P("tp", None), P("data", "tp"), P("tp")),
        out_specs=(P("data", "tp"), P("data", "tp")),
        check_vma=False,
    )
```

time: 88.1 us -> 85.8 us (0.974)
  local copies, waits for them, and re-layouts: 4.61 us -> 1.94 us
    unnamed x2, local copies, waits for them, and re-layouts: 4.61 us -> 1.94 us
where the time goes in v2:
time: 85.8 us; the launch traced here: 85.6 us
  Pallas kernels  83 us (97%)
  local copies, waits for them, and re-layouts  1.94 us (2%)
    pallas_call x1, Pallas kernels, local_step(): pl.pallas_call(functools.partial(kernel, tp, tok_rows, d_local), out_shap...  83 us
    unnamed x2, local copies, waits for them, and re-layouts  1.94 us

profile of v2, /device:TPU:81, one launch (start us, length us, event | category | flops | bytes accessed | tf_op | source)
XLA Modules:
  0.0 85.6 jit_solution(14418760374467629115)
XLA Ops:
  0.6 83.0 %project_reduce_norm.1 = (bf16[256,2048]{1,0:T(8,128)(2,1)S(1)}, bf16[256,2048]{1,0:T(8,128)(2,1)S(1)}) custom-call(bf16[256,2048]{1,0:T(8,128)(2,1)} %a_hbm.1, bf16[2048,16384]{1,0:T(8,128)(2,1)} %w_hbm.1, bf16[256,2048]{1,0:T(8,128)(2,1)} %r_hbm.1, f32[1,2048]{1,0:T(1,128)} %bitcast.1), custom_call_target="tpu_custom_call" | custom-call | tf_op jit(solution)/shard_map/project_reduce_norm/pallas_call | solution.py:213
  83.7 1.0 %copy.8 = bf16[256,2048]{1,0:T(8,128)(2,1)} copy(bf16[256,2048]{1,0:T(8,128)(2,1)S(1)} %get-tuple-element.2) | data formatting | bytes 2097152
  84.6 1.0 %copy.9 = bf16[256,2048]{1,0:T(8,128)(2,1)} copy(bf16[256,2048]{1,0:T(8,128)(2,1)S(1)} %get-tuple-element.3) | data formatting | bytes 2097152

commit v3 on v2

v3 whole, which is shorter than its diff:
```python
import functools

import jax
import jax.numpy as jnp
from jax import lax
from jax.experimental import pallas as pl
from jax.experimental.pallas import tpu as pltpu
from jax.sharding import PartitionSpec as P

EPS = 1e-5
CORES = 2
COLS = 256
W_SLOTS = 6
ROWS = 128
OUT_ROWS = 64


def reduce_kernel(
    tp, d_local, a_hbm, w_hbm, r_hbm, g_hbm, hid, hid_bf, sq_sum, gain,
    a, w, part, recv, relay_out, relay_in, res, sq_all,
    a_sem, w_sem, r_sem, g_sem, send_sem, recv_sem, rsend_sem, rrecv_sem, qsend_sem, qrecv_sem,
):
    chips = tp // CORES
    half = d_local // 2
    pp = half // COLS
    blk = 4 * pp
    tok_rows = a.shape[0]
    blocks = tok_rows // ROWS
    me = lax.axis_index("tp")
    chip, core = me // CORES, me % CORES

    def w_col(g):
        s, i = g % 2, (g % blk) // 2
        b, p, ph = i % 2, i // 2, g // blk
        is0 = (3 - ph) * (2 - ph) * (1 - ph) // 6
        is1 = ph * (3 - ph) * (2 - ph) // 2
        is2 = ph * (3 - ph) * (ph - 1) // 2
        kept = ph // 2
        step = 2 * s - 1
        hop = is0 * 2 + is1 * step + kept * (1 - b) * step
        to_core = (1 - kept) * b + is2 * (1 - core) + (kept - is2) * core
        in_half = s + is1 * (1 - 2 * s)
        to = ((chip + chips + hop) % chips) * CORES + to_core
        return to * d_local + in_half * half + p * COLS

    def w_copy(g):
        slot = g % W_SLOTS
        cols = pl.ds(pl.multiple_of(w_col(g), COLS), COLS)
        return pltpu.make_async_copy(w_hbm.at[:, cols], w.at[slot], w_sem.at[slot])

    def number(p, b, s):
        return (2 * p + b) * 2 + s

    def piece_copy(g):
        s, b, ph = g % 2, (g // 2) % 2, g // blk
        far = 1 - ph // 2
        to_chip = (chip + chips + far * (2 * s - 1)) % chips
        to_core = far * b + (1 - far) * (1 - core)
        slot = g + far * (core - b) * 2
        return pltpu.make_async_remote_copy(
            src_ref=part.at[g],
            dst_ref=recv.at[slot],
            send_sem=send_sem.at[g],
            recv_sem=recv_sem.at[slot],
            device_id={"tp": to_chip * CORES + to_core},
            device_id_type=pl.DeviceIdType.MESH,
        )

    def recv_wait(slot):
        pltpu.make_async_copy(recv.at[slot], recv.at[slot], recv_sem.at[slot]).wait()

    def relay_copy(j):
        to_chip = (chip + chips + 2 * (j % 2) - 1) % chips
        return pltpu.make_async_remote_copy(
            src_ref=relay_out.at[j],
            dst_ref=relay_in.at[j],
            send_sem=rsend_sem.at[j],
            recv_sem=rrecv_sem.at[j],
            device_id={"tp": to_chip * CORES + core},
            device_id_type=pl.DeviceIdType.MESH,
        )

    def sq_copy(j):
        return pltpu.make_async_remote_copy(
            src_ref=sq_all.at[me],
            dst_ref=sq_all.at[me],
            send_sem=qsend_sem.at[j],
            recv_sem=qrecv_sem.at[me],
            device_id={"tp": (me + j) % tp},
            device_id_type=pl.DeviceIdType.MESH,
        )

    a_copy = pltpu.make_async_copy(a_hbm, a, a_sem)
    r_copy = pltpu.make_async_copy(r_hbm, res, r_sem)
    g_copy = pltpu.make_async_copy(g_hbm, gain, g_sem)
    a_copy.start()
    w_copy(0).start()
    barrier = pltpu.get_barrier_semaphore()
    near = [chip * CORES + 1 - core]
    for hop in (1, chips - 1):
        near += [((chip + hop) % chips) * CORES + b for b in range(CORES)]
    for peer in near:
        pl.semaphore_signal(
            barrier, inc=1, device_id={"tp": peer}, device_id_type=pl.DeviceIdType.MESH
        )
    for g in range(1, W_SLOTS):
        w_copy(g).start()
    a_copy.wait()

    def project(g, carry):
        slot = g % W_SLOTS
        w_copy(g).wait()
        part[g] = jnp.dot(a[...], w[slot], preferred_element_type=jnp.float32).astype(jnp.bfloat16)

        @pl.when(g == 0)
        def _():
            pl.semaphore_wait(barrier, len(near))

        @pl.when(g < 3 * blk)
        def _():
            piece_copy(g).start()

        @pl.when(g + W_SLOTS < 4 * blk)
        def _():
            w_copy(g + W_SLOTS).start()

        return carry

    lax.fori_loop(0, 4 * blk, project, 0)
    r_copy.start()
    g_copy.start()

    def relay_wait(p, carry):
        for s in range(2):
            recv_wait(number(p, 0, s))
            recv_wait(number(p, 1, s))
            recv_wait(2 * blk + number(p, 0, s))
        return carry

    lax.fori_loop(0, pp, relay_wait, 0)

    def row_block(rb):
        return pl.ds(pl.multiple_of(rb * ROWS, ROWS), ROWS)

    def relay(j, carry):
        rows, s = row_block(j // 2), j % 2
        for p in range(pp):
            relay_out[j, :, p * COLS : (p + 1) * COLS] = (
                recv[number(p, 0, s), rows].astype(jnp.float32)
                + recv[number(p, 1, s), rows].astype(jnp.float32)
                + recv[2 * blk + number(p, 0, s), rows].astype(jnp.float32)
                + part[3 * blk + number(p, 0, s), rows].astype(jnp.float32)
            )
        relay_copy(j).start()
        return carry

    lax.fori_loop(0, 2 * blocks, relay, 0)
    r_copy.wait()

    def gather(i, carry):
        p, s = i // 2, i % 2
        cols = pl.ds(pl.multiple_of(s * half + p * COLS, COLS), COLS)
        direct = [blk + number(p, b, 1 - s) for b in range(CORES)]
        own = number(p, 1, s)
        for slot in direct:
            recv_wait(slot)
        recv_wait(2 * blk + own)
        hid[:, cols] = (
            res[:, cols].astype(jnp.float32)
            + part[3 * blk + own].astype(jnp.float32)
            + recv[2 * blk + own].astype(jnp.float32)
            + recv[direct[0]].astype(jnp.float32)
            + recv[direct[1]].astype(jnp.float32)
        )
        return carry

    lax.fori_loop(0, 2 * pp, gather, 0)

    for rb in range(blocks):
        rows = slice(rb * ROWS, (rb + 1) * ROWS)
        total = jnp.zeros((ROWS, 128), jnp.float32)
        for s in range(2):
            relay_copy(2 * rb + s).wait_recv()
            for c in range(0, half, 128):
                cols = slice(s * half + c, s * half + c + 128)
                h = hid[rows, cols] + relay_in[2 * rb + s, :, c : c + 128]
                hid[rows, cols] = h
                hid_bf[rows, cols] = h.astype(jnp.bfloat16)
                total += h * h
        sq_all[me, :, rows] = jnp.sum(jnp.transpose(total).reshape(16, 8, ROWS), axis=0)
    for j in range(1, tp):
        sq_copy(j).start()

    def drain(g, carry):
        piece_copy(g).wait_send()
        return carry

    lax.fori_loop(0, 3 * blk, drain, 0)
    for j in range(2 * blocks):
        relay_copy(j).wait_send()
    g_copy.wait()
    for j in range(1, tp):
        peer = (me + j) % tp
        pltpu.make_async_copy(sq_all.at[peer], sq_all.at[peer], qrecv_sem.at[peer]).wait()
    sq_sum[...] = jnp.sum(sq_all[...], axis=0)
    for j in range(1, tp):
        sq_copy(j).wait_send()


def norm_kernel(d_model, hid, hid_bf, sq_sum, gain, hid_out, nrm_out, nrm, sem):
    tok_rows, d_local = hid.shape
    hid_copy = pltpu.make_async_copy(hid_bf, hid_out, sem.at[0])
    hid_copy.start()
    sq_total = jnp.sum(sq_sum[...], axis=0, keepdims=True)
    scale_row = lax.rsqrt(sq_total / d_model + EPS)
    scale = jnp.transpose(jnp.broadcast_to(scale_row, (128, tok_rows)))
    copies = [hid_copy]
    for i, row in enumerate(range(0, tok_rows, OUT_ROWS)):
        rows = slice(row, row + OUT_ROWS)
        for c in range(0, d_local, 128):
            cols = slice(c, c + 128)
            nrm[rows, cols] = (hid[rows, cols] * scale[rows] * gain[:, cols]).astype(jnp.bfloat16)
        copies.append(pltpu.make_async_copy(nrm.at[rows], nrm_out.at[rows], sem.at[1 + i]))
        copies[-1].start()
    for copy in copies:
        copy.wait()


def solution(mesh):
    tp = mesh.shape["tp"]

    def local_step(attn_blk, w_blk, resid_blk, gain_blk):
        tok_rows, depth = attn_blk.shape
        d_local = resid_blk.shape[1]
        pp = d_local // 2 // COLS
        blocks = tok_rows // ROWS
        f32, bf16 = jnp.float32, jnp.bfloat16
        piece = (tok_rows, COLS)
        dma = pltpu.SemaphoreType.DMA
        hbm = pl.BlockSpec(memory_space=pl.ANY)
        vmem = pl.BlockSpec(memory_space=pltpu.VMEM)
        held = pl.pallas_call(
            functools.partial(reduce_kernel, tp, d_local),
            out_shape=[
                pltpu.VMEM((tok_rows, d_local), f32),
                pltpu.VMEM((tok_rows, d_local), bf16),
                pltpu.VMEM((8, tok_rows), f32),
                pltpu.VMEM((1, d_local), f32),
            ],
            in_specs=[hbm] * 4,
            out_specs=[vmem] * 4,
            scratch_shapes=[
                pltpu.VMEM((tok_rows, depth), bf16),
                pltpu.VMEM((W_SLOTS, depth, COLS), bf16),
                pltpu.VMEM((16 * pp, *piece), bf16),
                pltpu.VMEM((12 * pp, *piece), bf16),
                pltpu.VMEM((2 * blocks, ROWS, d_local // 2), f32),
                pltpu.VMEM((2 * blocks, ROWS, d_local // 2), f32),
                pltpu.VMEM((tok_rows, d_local), bf16),
                pltpu.VMEM((tp, 8, tok_rows), f32),
                dma,
                dma((W_SLOTS,)),
                dma,
                dma,
                dma((12 * pp,)),
                dma((12 * pp,)),
                dma((2 * blocks,)),
                dma((2 * blocks,)),
                dma((tp,)),
                dma((tp,)),
            ],
            compiler_params=pltpu.CompilerParams(
                collective_id=0, has_side_effects=True, vmem_limit_bytes=52 * 2**20
            ),
            name="project_reduce",
        )(attn_blk, w_blk, resid_blk, gain_blk.reshape(1, d_local))
        return pl.pallas_call(
            functools.partial(norm_kernel, tp * d_local),
            out_shape=[jax.ShapeDtypeStruct((tok_rows, d_local), bf16)] * 2,
            in_specs=[vmem] * 4,
            out_specs=[hbm] * 2,
            scratch_shapes=[
                pltpu.VMEM((tok_rows, d_local), bf16),
                dma((1 + tok_rows // OUT_ROWS,)),
            ],
            compiler_params=pltpu.CompilerParams(vmem_limit_bytes=16 * 2**20),
            name="norm_write",
        )(*held)

    return jax.shard_map(
        local_step,
        mesh=mesh,
        in_specs=(P("data", "tp"), P("tp", None), P("data", "tp"), P("tp")),
        out_specs=(P("data", "tp"), P("data", "tp")),
        check_vma=False,
    )
```

time: 85.8 us -> 81.2 us (0.946)
  Pallas kernels: 83 us -> 80.5 us
  local copies, waits for them, and re-layouts: 1.94 us -> 0 us
    pallas_call x1 -> x2, Pallas kernels: 83 us -> 80.5 us  [the longest x1 79.1 us: local_step(): pl.pallas_call(functools.partial(reduce_kernel, tp, d_local), out_shape=[...]
    unnamed x2 -> x0, local copies, waits for them, and re-layouts: 1.94 us -> none
where the time goes in v3:
time: 81.2 us; the launch traced here: 81.1 us
  Pallas kernels  80.5 us (99%)
    pallas_call x1, Pallas kernels, local_step(): pl.pallas_call(functools.partial(reduce_kernel, tp, d_local), out_shape=[...  79.1 us

profile of v3, /device:TPU:81, one launch (start us, length us, event | category | flops | bytes accessed | tf_op | source)
XLA Modules:
  0.0 81.1 jit_solution(17378213116920201047)
XLA Ops:
  0.6 79.1 %project_reduce.1 = (f32[256,2048]{1,0:T(8,128)S(1)}, bf16[256,2048]{1,0:T(8,128)(2,1)S(1)}, f32[8,256]{1,0:T(8,128)S(1)}, f32[1,2048]{1,0:T(1,128)S(1)}) custom-call(bf16[256,2048]{1,0:T(8,128)(2,1)} %a_hbm.1, bf16[2048,16384]{1,0:T(8,128)(2,1)} %w_hbm.1, bf16[256,2048]{1,0:T(8,128)(2,1)} %r_hbm.1, f32[1,2048]{1,0:T(1,128)} %bitcast.1), custom_call_target="tpu_custom_call" | custom-call | tf_op jit(solution)/shard_map/project_reduce/pallas_call | solution.py:242
  79.8 1.4 %norm_write.1 = (bf16[256,2048]{1,0:T(8,128)(2,1)}, bf16[256,2048]{1,0:T(8,128)(2,1)}) custom-call(f32[256,2048]{1,0:T(8,128)S(1)} %get-tuple-element.6.hid, bf16[256,2048]{1,0:T(8,128)(2,1)S(1)} %get-tuple-element.7.hid_bf, f32[8,256]{1,0:T(8,128)S(1)} %get-tuple-element.8.sq_sum, f32[1,2048]{1,0:T(1,128)S(1)} %get-tuple-element.9.gain), custom_call_target="tpu_custom_call" | custom-call | tf_op jit(solution)/shard_map/norm_write/pallas_call | solution.py:277

commit v4 on v3

--- a/solution.py
+++ b/solution.py
@@ -11,14 +11,14 @@
 CORES = 2
 COLS = 256
 W_SLOTS = 6
-ROWS = 128
+ROWS = 64
 OUT_ROWS = 64
 
 
 def reduce_kernel(
     tp, d_local, a_hbm, w_hbm, r_hbm, g_hbm, hid, hid_bf, sq_sum, gain,
     a, w, part, recv, relay_out, relay_in, res, sq_all,
-    a_sem, w_sem, r_sem, g_sem, send_sem, recv_sem, rsend_sem, rrecv_sem, qsend_sem, qrecv_sem,
+    a_sem, w_sem, r_sem, g_sem, send_sem, mid_sem, end_sem, rsend_sem, rrecv_sem, q_sem,
 ):
     chips = tp // CORES
     half = d_local // 2
@@ -38,7 +38,8 @@
         kept = ph // 2
         step = 2 * s - 1
         hop = is0 * 2 + is1 * step + kept * (1 - b) * step
-        to_core = (1 - kept) * b + is2 * (1 - core) + (kept - is2) * core
+        mine = (kept - is2) * b + is2 * (1 - b)
+        to_core = (1 - kept) * b + kept * (mine * core + (1 - mine) * (1 - core))
         in_half = s + is1 * (1 - 2 * s)
         to = ((chip + chips + hop) % chips) * CORES + to_core
         return to * d_local + in_half * half + p * COLS
@@ -51,32 +52,33 @@
     def number(p, b, s):
         return (2 * p + b) * 2 + s
 
-    def piece_copy(g):
+    def piece_copy(g, sem, rows=slice(None)):
         s, b, ph = g % 2, (g // 2) % 2, g // blk
         far = 1 - ph // 2
+        direct = far * ph
         to_chip = (chip + chips + far * (2 * s - 1)) % chips
-        to_core = far * b + (1 - far) * (1 - core)
+        to_core = direct * b + (far - direct) * (1 - b) + (1 - far) * (1 - core)
         slot = g + far * (core - b) * 2
         return pltpu.make_async_remote_copy(
-            src_ref=part.at[g],
-            dst_ref=recv.at[slot],
-            send_sem=send_sem.at[g],
-            recv_sem=recv_sem.at[slot],
+            src_ref=part.at[g, rows],
+            dst_ref=recv.at[slot, rows],
+            send_sem=send_sem,
+            recv_sem=sem,
             device_id={"tp": to_chip * CORES + to_core},
             device_id_type=pl.DeviceIdType.MESH,
         )
 
-    def recv_wait(slot):
-        pltpu.make_async_copy(recv.at[slot], recv.at[slot], recv_sem.at[slot]).wait()
+    def wait_for(ref, sem):
+        pltpu.make_async_copy(ref, ref, sem).wait()
 
     def relay_copy(j):
         to_chip = (chip + chips + 2 * (j % 2) - 1) % chips
         return pltpu.make_async_remote_copy(
             src_ref=relay_out.at[j],
             dst_ref=relay_in.at[j],
-            send_sem=rsend_sem.at[j],
+            send_sem=rsend_sem,
             recv_sem=rrecv_sem.at[j],
-            device_id={"tp": to_chip * CORES + core},
+            device_id={"tp": to_chip * CORES + 1 - core},
             device_id_type=pl.DeviceIdType.MESH,
         )
 
@@ -84,17 +86,23 @@
         return pltpu.make_async_remote_copy(
             src_ref=sq_all.at[me],
             dst_ref=sq_all.at[me],
-            send_sem=qsend_sem.at[j],
-            recv_sem=qrecv_sem.at[me],
+            send_sem=q_sem.at[0],
+            recv_sem=q_sem.at[1],
             device_id={"tp": (me + j) % tp},
             device_id_type=pl.DeviceIdType.MESH,
         )
 
-    a_copy = pltpu.make_async_copy(a_hbm, a, a_sem)
+    top, low = slice(0, tok_rows // 2), slice(tok_rows // 2, tok_rows)
+    a_copies = [
+        pltpu.make_async_copy(a_hbm.at[rows], a.at[rows], a_sem.at[i])
+        for i, rows in enumerate((top, low))
+    ]
     r_copy = pltpu.make_async_copy(r_hbm, res, r_sem)
     g_copy = pltpu.make_async_copy(g_hbm, gain, g_sem)
-    a_copy.start()
+    a_copies[0].start()
     w_copy(0).start()
+    w_copy(1).start()
+    a_copies[1].start()
     barrier = pltpu.get_barrier_semaphore()
     near = [chip * CORES + 1 - core]
     for hop in (1, chips - 1):
@@ -103,22 +111,39 @@
         pl.semaphore_signal(
             barrier, inc=1, device_id={"tp": peer}, device_id_type=pl.DeviceIdType.MESH
         )
-    for g in range(1, W_SLOTS):
+    for g in range(2, W_SLOTS):
         w_copy(g).start()
-    a_copy.wait()
-
-    def project(g, carry):
-        slot = g % W_SLOTS
+
+    def project(g, rows=slice(None)):
+        part[g, rows] = jnp.dot(
+            a[rows], w[g % W_SLOTS], preferred_element_type=jnp.float32
+        ).astype(jnp.bfloat16)
+
+    for i, rows in enumerate((top, low)):
+        a_copies[i].wait()
+        for g in range(2):
+            if i == 0:
+                w_copy(g).wait()
+            project(g, rows)
+            if i == 0 and g == 0:
+                pl.semaphore_wait(barrier, len(near))
+            piece_copy(g, mid_sem, rows).start()
+    for g in range(2):
+        w_copy(W_SLOTS + g).start()
+
+    def step(g, carry):
         w_copy(g).wait()
-        part[g] = jnp.dot(a[...], w[slot], preferred_element_type=jnp.float32).astype(jnp.bfloat16)
-
-        @pl.when(g == 0)
+        project(g)
+        b, ph = (g // 2) % 2, g // blk
+        for_end = ph % 2 + ph // 2 * b
+
+        @pl.when((g < 3 * blk) & (for_end == 0))
         def _():
-            pl.semaphore_wait(barrier, len(near))
-
-        @pl.when(g < 3 * blk)
+            piece_copy(g, mid_sem).start()
+
+        @pl.when((g < 3 * blk) & (for_end == 1))
         def _():
-            piece_copy(g).start()
+            piece_copy(g, end_sem).start()
 
         @pl.when(g + W_SLOTS < 4 * blk)
         def _():
@@ -126,18 +151,10 @@
 
         return carry
 
-    lax.fori_loop(0, 4 * blk, project, 0)
+    lax.fori_loop(2, 4 * blk, step, 0)
     r_copy.start()
     g_copy.start()
-
-    def relay_wait(p, carry):
-        for s in range(2):
-            recv_wait(number(p, 0, s))
-            recv_wait(number(p, 1, s))
-            recv_wait(2 * blk + number(p, 0, s))
-        return carry
-
-    lax.fori_loop(0, pp, relay_wait, 0)
+    wait_for(recv.at[pl.ds(0, blk + blk // 2)], mid_sem)
 
     def row_block(rb):
         return pl.ds(pl.multiple_of(rb * ROWS, ROWS), ROWS)
@@ -156,15 +173,13 @@
 
     lax.fori_loop(0, 2 * blocks, relay, 0)
     r_copy.wait()
+    wait_for(recv.at[pl.ds(0, blk + blk // 2)], end_sem)
 
     def gather(i, carry):
         p, s = i // 2, i % 2
         cols = pl.ds(pl.multiple_of(s * half + p * COLS, COLS), COLS)
         direct = [blk + number(p, b, 1 - s) for b in range(CORES)]
         own = number(p, 1, s)
-        for slot in direct:
-            recv_wait(slot)
-        recv_wait(2 * blk + own)
         hid[:, cols] = (
             res[:, cols].astype(jnp.float32)
             + part[3 * blk + own].astype(jnp.float32)
@@ -176,6 +191,7 @@
 
     lax.fori_loop(0, 2 * pp, gather, 0)
 
+    totals = []
     for rb in range(blocks):
         rows = slice(rb * ROWS, (rb + 1) * ROWS)
         total = jnp.zeros((ROWS, 128), jnp.float32)
@@ -185,26 +201,29 @@
                 cols = slice(s * half + c, s * half + c + 128)
                 h = hid[rows, cols] + relay_in[2 * rb + s, :, c : c + 128]
                 hid[rows, cols] = h
-                hid_bf[rows, cols] = h.astype(jnp.bfloat16)
                 total += h * h
-        sq_all[me, :, rows] = jnp.sum(jnp.transpose(total).reshape(16, 8, ROWS), axis=0)
+        totals.append(total)
+        if len(totals) * ROWS == 128:
+            by_lane = jnp.transpose(jnp.concatenate(totals, axis=0))
+            sq_all[me, :, (rb + 1) * ROWS - 128 : (rb + 1) * ROWS] = jnp.sum(
+                by_lane.reshape(16, 8, 128), axis=0
+            )
+            totals = []
     for j in range(1, tp):
         sq_copy(j).start()
 
-    def drain(g, carry):
-        piece_copy(g).wait_send()
+    def narrow(rb, carry):
+        rows = row_block(rb)
+        hid_bf[rows] = hid[rows].astype(jnp.bfloat16)
         return carry
 
-    lax.fori_loop(0, 3 * blk, drain, 0)
-    for j in range(2 * blocks):
-        relay_copy(j).wait_send()
+    lax.fori_loop(0, blocks, narrow, 0)
+    wait_for(part.at[pl.ds(0, 3 * blk)], send_sem)
+    wait_for(relay_out, rsend_sem)
     g_copy.wait()
-    for j in range(1, tp):
-        peer = (me + j) % tp
-        pltpu.make_async_copy(sq_all.at[peer], sq_all.at[peer], qrecv_sem.at[peer]).wait()
+    wait_for(sq_all.at[pl.ds(0, tp - 1)], q_sem.at[1])
     sq_sum[...] = jnp.sum(sq_all[...], axis=0)
-    for j in range(1, tp):
-        sq_copy(j).wait_send()
+    wait_for(sq_all.at[pl.ds(0, tp - 1)], q_sem.at[0])
 
 
 def norm_kernel(d_model, hid, hid_bf, sq_sum, gain, hid_out, nrm_out, nrm, sem):
@@ -258,16 +277,16 @@
                 pltpu.VMEM((2 * blocks, ROWS, d_local // 2), f32),
                 pltpu.VMEM((tok_rows, d_local), bf16),
                 pltpu.VMEM((tp, 8, tok_rows), f32),
-                dma,
+                dma((2,)),
                 dma((W_SLOTS,)),
                 dma,
                 dma,
-                dma((12 * pp,)),
-                dma((12 * pp,)),
+                dma,
+                dma,
+                dma,
+                dma,
                 dma((2 * blocks,)),
-                dma((2 * blocks,)),
-                dma((tp,)),
-                dma((tp,)),
+                dma((2,)),
             ],
             compiler_params=pltpu.CompilerParams(
                 collective_id=0, has_side_effects=True, vmem_limit_bytes=52 * 2**20

time: 81.2 us -> 79.6 us (0.980)
  Pallas kernels: 80.5 us -> 78.9 us
    pallas_call x1, Pallas kernels: 79.1 us -> 77.5 us  [local_step(): pl.pallas_call(functools.partial(reduce_kernel, tp, d_local), out_shape=[...]
where the time goes in v4:
time: 79.6 us; the launch traced here: 79.5 us
  Pallas kernels  78.9 us (99%)
    pallas_call x1, Pallas kernels, local_step(): pl.pallas_call(functools.partial(reduce_kernel, tp, d_local), out_shape=[...  77.5 us

profile of v4, /device:TPU:81, one launch (start us, length us, event | category | flops | bytes accessed | tf_op | source)
XLA Modules:
  0.0 79.5 jit_solution(3679096528478439066)
XLA Ops:
  0.6 77.5 %project_reduce.1 = (f32[256,2048]{1,0:T(8,128)S(1)}, bf16[256,2048]{1,0:T(8,128)(2,1)S(1)}, f32[8,256]{1,0:T(8,128)S(1)}, f32[1,2048]{1,0:T(1,128)S(1)}) custom-call(bf16[256,2048]{1,0:T(8,128)(2,1)} %a_hbm.1, bf16[2048,16384]{1,0:T(8,128)(2,1)} %w_hbm.1, bf16[256,2048]{1,0:T(8,128)(2,1)} %r_hbm.1, f32[1,2048]{1,0:T(1,128)} %bitcast.1), custom_call_target="tpu_custom_call" | custom-call | tf_op jit(solution)/shard_map/project_reduce/pallas_call | solution.py:261
  78.2 1.4 %norm_write.1 = (bf16[256,2048]{1,0:T(8,128)(2,1)}, bf16[256,2048]{1,0:T(8,128)(2,1)}) custom-call(f32[256,2048]{1,0:T(8,128)S(1)} %get-tuple-element.6.hid, bf16[256,2048]{1,0:T(8,128)(2,1)S(1)} %get-tuple-element.7.hid_bf, f32[8,256]{1,0:T(8,128)S(1)} %get-tuple-element.8.sq_sum, f32[1,2048]{1,0:T(1,128)S(1)} %get-tuple-element.9.gain), custom_call_target="tpu_custom_call" | custom-call | tf_op jit(solution)/shard_map/norm_write/pallas_call | solution.py:296

commit v5 on v4

--- a/solution.py
+++ b/solution.py
@@ -36,7 +36,7 @@
         is1 = ph * (3 - ph) * (2 - ph) // 2
         is2 = ph * (3 - ph) * (ph - 1) // 2
         kept = ph // 2
-        step = 2 * s - 1
+        step = 1 - 2 * s
         hop = is0 * 2 + is1 * step + kept * (1 - b) * step
         mine = (kept - is2) * b + is2 * (1 - b)
         to_core = (1 - kept) * b + kept * (mine * core + (1 - mine) * (1 - core))
@@ -56,7 +56,7 @@
         s, b, ph = g % 2, (g // 2) % 2, g // blk
         far = 1 - ph // 2
         direct = far * ph
-        to_chip = (chip + chips + far * (2 * s - 1)) % chips
+        to_chip = (chip + chips + far * (1 - 2 * s)) % chips
         to_core = direct * b + (far - direct) * (1 - b) + (1 - far) * (1 - core)
         slot = g + far * (core - b) * 2
         return pltpu.make_async_remote_copy(
@@ -72,7 +72,7 @@
         pltpu.make_async_copy(ref, ref, sem).wait()
 
     def relay_copy(j):
-        to_chip = (chip + chips + 2 * (j % 2) - 1) % chips
+        to_chip = (chip + chips + 1 - 2 * (j % 2)) % chips
         return pltpu.make_async_remote_copy(
             src_ref=relay_out.at[j],
             dst_ref=relay_in.at[j],
@@ -82,13 +82,19 @@
             device_id_type=pl.DeviceIdType.MESH,
         )
 
-    def sq_copy(j):
+    def peers(hops):
+        return [((chip + hop) % chips) * CORES + b for hop in hops for b in range(CORES)]
+
+    partner = chip * CORES + 1 - core
+    others = sorted(range(1, chips), key=lambda hop: -min(hop, chips - hop))
+
+    def sq_copy(peer):
         return pltpu.make_async_remote_copy(
             src_ref=sq_all.at[me],
             dst_ref=sq_all.at[me],
             send_sem=q_sem.at[0],
             recv_sem=q_sem.at[1],
-            device_id={"tp": (me + j) % tp},
+            device_id={"tp": peer},
             device_id_type=pl.DeviceIdType.MESH,
         )
 
@@ -99,18 +105,16 @@
     ]
     r_copy = pltpu.make_async_copy(r_hbm, res, r_sem)
     g_copy = pltpu.make_async_copy(g_hbm, gain, g_sem)
+    barrier = pltpu.get_barrier_semaphore()
+    near = peers((1, chips - 1)) + [partner]
+    for peer in near:
+        pl.semaphore_signal(
+            barrier, inc=1, device_id={"tp": peer}, device_id_type=pl.DeviceIdType.MESH
+        )
     a_copies[0].start()
     w_copy(0).start()
     w_copy(1).start()
     a_copies[1].start()
-    barrier = pltpu.get_barrier_semaphore()
-    near = [chip * CORES + 1 - core]
-    for hop in (1, chips - 1):
-        near += [((chip + hop) % chips) * CORES + b for b in range(CORES)]
-    for peer in near:
-        pl.semaphore_signal(
-            barrier, inc=1, device_id={"tp": peer}, device_id_type=pl.DeviceIdType.MESH
-        )
     for g in range(2, W_SLOTS):
         w_copy(g).start()
 
@@ -206,11 +210,11 @@
         if len(totals) * ROWS == 128:
             by_lane = jnp.transpose(jnp.concatenate(totals, axis=0))
             sq_all[me, :, (rb + 1) * ROWS - 128 : (rb + 1) * ROWS] = jnp.sum(
-                by_lane.reshape(16, 8, 128), axis=0
+                by_lane, axis=0, keepdims=True
             )
             totals = []
-    for j in range(1, tp):
-        sq_copy(j).start()
+    for peer in peers(others) + [partner]:
+        sq_copy(peer).start()
 
     def narrow(rb, carry):
         rows = row_block(rb)
@@ -230,8 +234,7 @@
     tok_rows, d_local = hid.shape
     hid_copy = pltpu.make_async_copy(hid_bf, hid_out, sem.at[0])
     hid_copy.start()
-    sq_total = jnp.sum(sq_sum[...], axis=0, keepdims=True)
-    scale_row = lax.rsqrt(sq_total / d_model + EPS)
+    scale_row = lax.rsqrt(sq_sum[...] / d_model + EPS)
     scale = jnp.transpose(jnp.broadcast_to(scale_row, (128, tok_rows)))
     copies = [hid_copy]
     for i, row in enumerate(range(0, tok_rows, OUT_ROWS)):
@@ -263,7 +266,7 @@
             out_shape=[
                 pltpu.VMEM((tok_rows, d_local), f32),
                 pltpu.VMEM((tok_rows, d_local), bf16),
-                pltpu.VMEM((8, tok_rows), f32),
+                pltpu.VMEM((1, tok_rows), f32),
                 pltpu.VMEM((1, d_local), f32),
             ],
             in_specs=[hbm] * 4,
@@ -276,7 +279,7 @@
                 pltpu.VMEM((2 * blocks, ROWS, d_local // 2), f32),
                 pltpu.VMEM((2 * blocks, ROWS, d_local // 2), f32),
                 pltpu.VMEM((tok_rows, d_local), bf16),
-                pltpu.VMEM((tp, 8, tok_rows), f32),
+                pltpu.VMEM((tp, 1, tok_rows), f32),
                 dma((2,)),
                 dma((W_SLOTS,)),
                 dma,

time: 79.6 us -> 81 us (1.018)
  Pallas kernels: 78.9 us -> 80.2 us
    pallas_call x1, Pallas kernels: 77.5 us -> 78.9 us  [local_step(): pl.pallas_call(functools.partial(reduce_kernel, tp, d_local), out_shape=[...]
where the time goes in v5:
time: 81 us; the launch traced here: 80.9 us
  Pallas kernels  80.2 us (99%)
    pallas_call x1, Pallas kernels, local_step(): pl.pallas_call(functools.partial(reduce_kernel, tp, d_local), out_shape=[...  78.9 us

profile of v5, /device:TPU:81, one launch (start us, length us, event | category | flops | bytes accessed | tf_op | source)
XLA Modules:
  0.0 80.9 jit_solution(8878798930841957588)
XLA Ops:
  0.6 78.9 %project_reduce.1 = (f32[256,2048]{1,0:T(8,128)S(1)}, bf16[256,2048]{1,0:T(8,128)(2,1)S(1)}, f32[1,256]{1,0:T(1,128)S(1)}, f32[1,2048]{1,0:T(1,128)S(1)}) custom-call(bf16[256,2048]{1,0:T(8,128)(2,1)} %a_hbm.1, bf16[2048,16384]{1,0:T(8,128)(2,1)} %w_hbm.1, bf16[256,2048]{1,0:T(8,128)(2,1)} %r_hbm.1, f32[1,2048]{1,0:T(1,128)} %bitcast.1), custom_call_target="tpu_custom_call" | custom-call | tf_op jit(solution)/shard_map/project_reduce/pallas_call | solution.py:264
  79.5 1.4 %norm_write.1 = (bf16[256,2048]{1,0:T(8,128)(2,1)}, bf16[256,2048]{1,0:T(8,128)(2,1)}) custom-call(f32[256,2048]{1,0:T(8,128)S(1)} %get-tuple-element.6.hid, bf16[256,2048]{1,0:T(8,128)(2,1)S(1)} %get-tuple-element.7.hid_bf, f32[1,256]{1,0:T(1,128)S(1)} %get-tuple-element.8.sq_sum, f32[1,2048]{1,0:T(1,128)S(1)} %get-tuple-element.9.gain), custom_call_target="tpu_custom_call" | custom-call | tf_op jit(solution)/shard_map/norm_write/pallas_call | solution.py:299

commit v6 on v5

--- a/solution.py
+++ b/solution.py
@@ -24,6 +24,7 @@
     half = d_local // 2
     pp = half // COLS
     blk = 4 * pp
+    mix = COLS // 2
     tok_rows = a.shape[0]
     blocks = tok_rows // ROWS
     me = lax.axis_index("tp")
@@ -36,7 +37,7 @@
         is1 = ph * (3 - ph) * (2 - ph) // 2
         is2 = ph * (3 - ph) * (ph - 1) // 2
         kept = ph // 2
-        step = 1 - 2 * s
+        step = 2 * s - 1
         hop = is0 * 2 + is1 * step + kept * (1 - b) * step
         mine = (kept - is2) * b + is2 * (1 - b)
         to_core = (1 - kept) * b + kept * (mine * core + (1 - mine) * (1 - core))
@@ -49,19 +50,29 @@
         cols = pl.ds(pl.multiple_of(w_col(g), COLS), COLS)
         return pltpu.make_async_copy(w_hbm.at[:, cols], w.at[slot], w_sem.at[slot])
 
+    def mixed_copies(i):
+        return [
+            pltpu.make_async_copy(
+                w_hbm.at[:, pl.ds(pl.multiple_of(w_col(g) + i * mix, mix), mix)],
+                w.at[i, :, pl.ds(g * mix, mix)],
+                w_sem.at[i],
+            )
+            for g in range(2)
+        ]
+
     def number(p, b, s):
         return (2 * p + b) * 2 + s
 
-    def piece_copy(g, sem, rows=slice(None)):
+    def piece_copy(g, sem, rows=slice(None), cols=slice(None)):
         s, b, ph = g % 2, (g // 2) % 2, g // blk
         far = 1 - ph // 2
         direct = far * ph
-        to_chip = (chip + chips + far * (1 - 2 * s)) % chips
+        to_chip = (chip + chips + far * (2 * s - 1)) % chips
         to_core = direct * b + (far - direct) * (1 - b) + (1 - far) * (1 - core)
         slot = g + far * (core - b) * 2
         return pltpu.make_async_remote_copy(
-            src_ref=part.at[g, rows],
-            dst_ref=recv.at[slot, rows],
+            src_ref=part.at[g, rows, cols],
+            dst_ref=recv.at[slot, rows, cols],
             send_sem=send_sem,
             recv_sem=sem,
             device_id={"tp": to_chip * CORES + to_core},
@@ -72,7 +83,7 @@
         pltpu.make_async_copy(ref, ref, sem).wait()
 
     def relay_copy(j):
-        to_chip = (chip + chips + 1 - 2 * (j % 2)) % chips
+        to_chip = (chip + chips + 2 * (j % 2) - 1) % chips
         return pltpu.make_async_remote_copy(
             src_ref=relay_out.at[j],
             dst_ref=relay_in.at[j],
@@ -105,39 +116,42 @@
     ]
     r_copy = pltpu.make_async_copy(r_hbm, res, r_sem)
     g_copy = pltpu.make_async_copy(g_hbm, gain, g_sem)
+    a_copies[0].start()
+    for copy in mixed_copies(0):
+        copy.start()
+    a_copies[1].start()
+    for copy in mixed_copies(1):
+        copy.start()
     barrier = pltpu.get_barrier_semaphore()
-    near = peers((1, chips - 1)) + [partner]
+    near = [partner] + peers((1, chips - 1))
     for peer in near:
         pl.semaphore_signal(
             barrier, inc=1, device_id={"tp": peer}, device_id_type=pl.DeviceIdType.MESH
         )
-    a_copies[0].start()
-    w_copy(0).start()
-    w_copy(1).start()
-    a_copies[1].start()
     for g in range(2, W_SLOTS):
         w_copy(g).start()
 
-    def project(g, rows=slice(None)):
-        part[g, rows] = jnp.dot(
-            a[rows], w[g % W_SLOTS], preferred_element_type=jnp.float32
-        ).astype(jnp.bfloat16)
-
-    for i, rows in enumerate((top, low)):
-        a_copies[i].wait()
-        for g in range(2):
+    for i in range(2):
+        for j, rows in enumerate((top, low)):
             if i == 0:
-                w_copy(g).wait()
-            project(g, rows)
-            if i == 0 and g == 0:
+                a_copies[j].wait()
+            if j == 0:
+                wait_for(w.at[i], w_sem.at[i])
+            quarter = jnp.dot(a[rows], w[i], preferred_element_type=jnp.float32)
+            for g in range(2):
+                cols = slice(i * mix, (i + 1) * mix)
+                part[g, rows, cols] = quarter[:, g * mix : (g + 1) * mix].astype(jnp.bfloat16)
+            if i == 0 and j == 0:
                 pl.semaphore_wait(barrier, len(near))
-            piece_copy(g, mid_sem, rows).start()
+            for g in range(2):
+                piece_copy(g, mid_sem, rows, cols).start()
     for g in range(2):
         w_copy(W_SLOTS + g).start()
 
     def step(g, carry):
+        slot = g % W_SLOTS
         w_copy(g).wait()
-        project(g)
+        part[g] = jnp.dot(a[...], w[slot], preferred_element_type=jnp.float32).astype(jnp.bfloat16)
         b, ph = (g // 2) % 2, g // blk
         for_end = ph % 2 + ph // 2 * b
 
@@ -232,18 +246,22 @@
 
 def norm_kernel(d_model, hid, hid_bf, sq_sum, gain, hid_out, nrm_out, nrm, sem):
     tok_rows, d_local = hid.shape
-    hid_copy = pltpu.make_async_copy(hid_bf, hid_out, sem.at[0])
-    hid_copy.start()
+    copies = []
+
+    def write(src, dst, rows):
+        copies.append(pltpu.make_async_copy(src.at[rows], dst.at[rows], sem.at[len(copies)]))
+        copies[-1].start()
+
+    blocks = [slice(row, row + OUT_ROWS) for row in range(0, tok_rows, OUT_ROWS)]
+    for rows in blocks:
+        write(hid_bf, hid_out, rows)
     scale_row = lax.rsqrt(sq_sum[...] / d_model + EPS)
     scale = jnp.transpose(jnp.broadcast_to(scale_row, (128, tok_rows)))
-    copies = [hid_copy]
-    for i, row in enumerate(range(0, tok_rows, OUT_ROWS)):
-        rows = slice(row, row + OUT_ROWS)
+    for rows in blocks:
         for c in range(0, d_local, 128):
             cols = slice(c, c + 128)
             nrm[rows, cols] = (hid[rows, cols] * scale[rows] * gain[:, cols]).astype(jnp.bfloat16)
-        copies.append(pltpu.make_async_copy(nrm.at[rows], nrm_out.at[rows], sem.at[1 + i]))
-        copies[-1].start()
+        write(nrm, nrm_out, rows)
     for copy in copies:
         copy.wait()
 
@@ -303,7 +321,7 @@
             out_specs=[hbm] * 2,
             scratch_shapes=[
                 pltpu.VMEM((tok_rows, d_local), bf16),
-                dma((1 + tok_rows // OUT_ROWS,)),
+                dma((2 * tok_rows // OUT_ROWS,)),
             ],
             compiler_params=pltpu.CompilerParams(vmem_limit_bytes=16 * 2**20),
             name="norm_write",

time: 81 us -> 79.6 us (0.983)
  Pallas kernels: 80.2 us -> 78.9 us
    pallas_call x1, Pallas kernels: 78.9 us -> 77.5 us  [local_step(): pl.pallas_call(functools.partial(reduce_kernel, tp, d_local), out_shape=[...]
where the time goes in v6:
time: 79.6 us; the launch traced here: 79.5 us
  Pallas kernels  78.9 us (99%)
    pallas_call x1, Pallas kernels, local_step(): pl.pallas_call(functools.partial(reduce_kernel, tp, d_local), out_shape=[...  77.5 us

profile of v6, /device:TPU:81, one launch (start us, length us, event | category | flops | bytes accessed | tf_op | source)
XLA Modules:
  0.0 79.5 jit_solution(4015696747777255122)
XLA Ops:
  0.6 77.5 %project_reduce.1 = (f32[256,2048]{1,0:T(8,128)S(1)}, bf16[256,2048]{1,0:T(8,128)(2,1)S(1)}, f32[1,256]{1,0:T(1,128)S(1)}, f32[1,2048]{1,0:T(1,128)S(1)}) custom-call(bf16[256,2048]{1,0:T(8,128)(2,1)} %a_hbm.1, bf16[2048,16384]{1,0:T(8,128)(2,1)} %w_hbm.1, bf16[256,2048]{1,0:T(8,128)(2,1)} %r_hbm.1, f32[1,2048]{1,0:T(1,128)} %bitcast.1), custom_call_target="tpu_custom_call" | custom-call | tf_op jit(solution)/shard_map/project_reduce/pallas_call | solution.py:282
  78.1 1.4 %norm_write.1 = (bf16[256,2048]{1,0:T(8,128)(2,1)}, bf16[256,2048]{1,0:T(8,128)(2,1)}) custom-call(f32[256,2048]{1,0:T(8,128)S(1)} %get-tuple-element.6.hid, bf16[256,2048]{1,0:T(8,128)(2,1)S(1)} %get-tuple-element.7.hid_bf, f32[1,256]{1,0:T(1,128)S(1)} %get-tuple-element.8.sq_sum, f32[1,2048]{1,0:T(1,128)S(1)} %get-tuple-element.9.gain), custom_call_target="tpu_custom_call" | custom-call | tf_op jit(solution)/shard_map/norm_write/pallas_call | solution.py:317

commit v7 on v5

--- a/solution.py
+++ b/solution.py
@@ -36,7 +36,7 @@
         is1 = ph * (3 - ph) * (2 - ph) // 2
         is2 = ph * (3 - ph) * (ph - 1) // 2
         kept = ph // 2
-        step = 1 - 2 * s
+        step = 2 * s - 1
         hop = is0 * 2 + is1 * step + kept * (1 - b) * step
         mine = (kept - is2) * b + is2 * (1 - b)
         to_core = (1 - kept) * b + kept * (mine * core + (1 - mine) * (1 - core))
@@ -56,7 +56,7 @@
         s, b, ph = g % 2, (g // 2) % 2, g // blk
         far = 1 - ph // 2
         direct = far * ph
-        to_chip = (chip + chips + far * (1 - 2 * s)) % chips
+        to_chip = (chip + chips + far * (2 * s - 1)) % chips
         to_core = direct * b + (far - direct) * (1 - b) + (1 - far) * (1 - core)
         slot = g + far * (core - b) * 2
         return pltpu.make_async_remote_copy(
@@ -72,7 +72,7 @@
         pltpu.make_async_copy(ref, ref, sem).wait()
 
     def relay_copy(j):
-        to_chip = (chip + chips + 1 - 2 * (j % 2)) % chips
+        to_chip = (chip + chips + 2 * (j % 2) - 1) % chips
         return pltpu.make_async_remote_copy(
             src_ref=relay_out.at[j],
             dst_ref=relay_in.at[j],
@@ -105,16 +105,16 @@
     ]
     r_copy = pltpu.make_async_copy(r_hbm, res, r_sem)
     g_copy = pltpu.make_async_copy(g_hbm, gain, g_sem)
-    barrier = pltpu.get_barrier_semaphore()
-    near = peers((1, chips - 1)) + [partner]
-    for peer in near:
-        pl.semaphore_signal(
-            barrier, inc=1, device_id={"tp": peer}, device_id_type=pl.DeviceIdType.MESH
-        )
     a_copies[0].start()
     w_copy(0).start()
     w_copy(1).start()
     a_copies[1].start()
+    barrier = pltpu.get_barrier_semaphore()
+    near = [partner] + peers((1, chips - 1))
+    for peer in near:
+        pl.semaphore_signal(
+            barrier, inc=1, device_id={"tp": peer}, device_id_type=pl.DeviceIdType.MESH
+        )
     for g in range(2, W_SLOTS):
         w_copy(g).start()
 
@@ -213,7 +213,8 @@
                 by_lane, axis=0, keepdims=True
             )
             totals = []
-    for peer in peers(others) + [partner]:
+    far_first = peers(others)
+    for peer in far_first[1::CORES] + [partner] + far_first[::CORES]:
         sq_copy(peer).start()
 
     def narrow(rb, carry):

time: 81 us -> 79.2 us (0.978)
  Pallas kernels: 80.2 us -> 78.4 us
    pallas_call x1, Pallas kernels: 78.9 us -> 77.1 us  [local_step(): pl.pallas_call(functools.partial(reduce_kernel, tp, d_local), out_shape=[...]
where the time goes in v7:
time: 79.2 us; the launch traced here: 79.1 us
  Pallas kernels  78.4 us (99%)
    pallas_call x1, Pallas kernels, local_step(): pl.pallas_call(functools.partial(reduce_kernel, tp, d_local), out_shape=[...  77.1 us

profile of v7, /device:TPU:81, one launch (start us, length us, event | category | flops | bytes accessed | tf_op | source)
XLA Modules:
  0.0 79.1 jit_solution(15990684392907331097)
XLA Ops:
  0.6 77.1 %project_reduce.1 = (f32[256,2048]{1,0:T(8,128)S(1)}, bf16[256,2048]{1,0:T(8,128)(2,1)S(1)}, f32[1,256]{1,0:T(1,128)S(1)}, f32[1,2048]{1,0:T(1,128)S(1)}) custom-call(bf16[256,2048]{1,0:T(8,128)(2,1)} %a_hbm.1, bf16[2048,16384]{1,0:T(8,128)(2,1)} %w_hbm.1, bf16[256,2048]{1,0:T(8,128)(2,1)} %r_hbm.1, f32[1,2048]{1,0:T(1,128)} %bitcast.1), custom_call_target="tpu_custom_call" | custom-call | tf_op jit(solution)/shard_map/project_reduce/pallas_call | solution.py:265
  77.7 1.4 %norm_write.1 = (bf16[256,2048]{1,0:T(8,128)(2,1)}, bf16[256,2048]{1,0:T(8,128)(2,1)}) custom-call(f32[256,2048]{1,0:T(8,128)S(1)} %get-tuple-element.6.hid, bf16[256,2048]{1,0:T(8,128)(2,1)S(1)} %get-tuple-element.7.hid_bf, f32[1,256]{1,0:T(1,128)S(1)} %get-tuple-element.8.sq_sum, f32[1,2048]{1,0:T(1,128)S(1)} %get-tuple-element.9.gain), custom_call_target="tpu_custom_call" | custom-call | tf_op jit(solution)/shard_map/norm_write/pallas_call | solution.py:300

commit v8 on v7

--- a/solution.py
+++ b/solution.py
@@ -10,15 +10,15 @@
 EPS = 1e-5
 CORES = 2
 COLS = 256
-W_SLOTS = 6
+W_SLOTS = 4
 ROWS = 64
-OUT_ROWS = 64
+OUT_ROWS = 128
 
 
 def reduce_kernel(
-    tp, d_local, a_hbm, w_hbm, r_hbm, g_hbm, hid, hid_bf, sq_sum, gain,
-    a, w, part, recv, relay_out, relay_in, res, sq_all,
-    a_sem, w_sem, r_sem, g_sem, send_sem, mid_sem, end_sem, rsend_sem, rrecv_sem, q_sem,
+    tp, d_local, a_hbm, w_hbm, r_hbm, g_hbm, hid, hid_bf, sq_all, gain,
+    a, w, part, recv, relay_out, relay_in, res,
+    a_sem, w_sem, send_sem, mid_sem, end_sem, rsend_sem, rrecv_sem, q_sem,
 ):
     chips = tp // CORES
     half = d_local // 2
@@ -71,13 +71,15 @@
     def wait_for(ref, sem):
         pltpu.make_async_copy(ref, ref, sem).wait()
 
-    def relay_copy(j):
+    early = 2 * (blocks - 1)
+
+    def relay_copy(j, sem):
         to_chip = (chip + chips + 2 * (j % 2) - 1) % chips
         return pltpu.make_async_remote_copy(
             src_ref=relay_out.at[j],
             dst_ref=relay_in.at[j],
             send_sem=rsend_sem,
-            recv_sem=rrecv_sem.at[j],
+            recv_sem=rrecv_sem.at[sem],
             device_id={"tp": to_chip * CORES + 1 - core},
             device_id_type=pl.DeviceIdType.MESH,
         )
@@ -103,14 +105,14 @@
         pltpu.make_async_copy(a_hbm.at[rows], a.at[rows], a_sem.at[i])
         for i, rows in enumerate((top, low))
     ]
-    r_copy = pltpu.make_async_copy(r_hbm, res, r_sem)
-    g_copy = pltpu.make_async_copy(g_hbm, gain, g_sem)
+    r_copy = pltpu.make_async_copy(r_hbm, res, a_sem.at[0])
+    g_copy = pltpu.make_async_copy(g_hbm, gain, a_sem.at[1])
     a_copies[0].start()
     w_copy(0).start()
     w_copy(1).start()
     a_copies[1].start()
     barrier = pltpu.get_barrier_semaphore()
-    near = [partner] + peers((1, chips - 1))
+    near = peers((1, chips - 1)) + [partner]
     for peer in near:
         pl.semaphore_signal(
             barrier, inc=1, device_id={"tp": peer}, device_id_type=pl.DeviceIdType.MESH
@@ -163,7 +165,7 @@
     def row_block(rb):
         return pl.ds(pl.multiple_of(rb * ROWS, ROWS), ROWS)
 
-    def relay(j, carry):
+    def relay(j, sem):
         rows, s = row_block(j // 2), j % 2
         for p in range(pp):
             relay_out[j, :, p * COLS : (p + 1) * COLS] = (
@@ -172,10 +174,15 @@
                 + recv[2 * blk + number(p, 0, s), rows].astype(jnp.float32)
                 + part[3 * blk + number(p, 0, s), rows].astype(jnp.float32)
             )
-        relay_copy(j).start()
+        relay_copy(j, sem).start()
+
+    def relay_early(j, carry):
+        relay(j, 0)
         return carry
 
-    lax.fori_loop(0, 2 * blocks, relay, 0)
+    lax.fori_loop(0, early, relay_early, 0)
+    for s in range(2):
+        relay(early + s, 1 + s)
     r_copy.wait()
     wait_for(recv.at[pl.ds(0, blk + blk // 2)], end_sem)
 
@@ -196,11 +203,13 @@
     lax.fori_loop(0, 2 * pp, gather, 0)
 
     totals = []
+    wait_for(relay_in.at[pl.ds(0, early)], rrecv_sem.at[0])
     for rb in range(blocks):
         rows = slice(rb * ROWS, (rb + 1) * ROWS)
         total = jnp.zeros((ROWS, 128), jnp.float32)
         for s in range(2):
-            relay_copy(2 * rb + s).wait_recv()
+            if rb == blocks - 1:
+                relay_copy(early + s, 1 + s).wait_recv()
             for c in range(0, half, 128):
                 cols = slice(s * half + c, s * half + c + 128)
                 h = hid[rows, cols] + relay_in[2 * rb + s, :, c : c + 128]
@@ -227,15 +236,14 @@
     wait_for(relay_out, rsend_sem)
     g_copy.wait()
     wait_for(sq_all.at[pl.ds(0, tp - 1)], q_sem.at[1])
-    sq_sum[...] = jnp.sum(sq_all[...], axis=0)
     wait_for(sq_all.at[pl.ds(0, tp - 1)], q_sem.at[0])
 
 
-def norm_kernel(d_model, hid, hid_bf, sq_sum, gain, hid_out, nrm_out, nrm, sem):
+def norm_kernel(d_model, hid, hid_bf, sq_all, gain, hid_out, nrm_out, nrm, sem):
     tok_rows, d_local = hid.shape
     hid_copy = pltpu.make_async_copy(hid_bf, hid_out, sem.at[0])
     hid_copy.start()
-    scale_row = lax.rsqrt(sq_sum[...] / d_model + EPS)
+    scale_row = lax.rsqrt(jnp.sum(sq_all[...], axis=0) / d_model + EPS)
     scale = jnp.transpose(jnp.broadcast_to(scale_row, (128, tok_rows)))
     copies = [hid_copy]
     for i, row in enumerate(range(0, tok_rows, OUT_ROWS)):
@@ -267,7 +275,7 @@
             out_shape=[
                 pltpu.VMEM((tok_rows, d_local), f32),
                 pltpu.VMEM((tok_rows, d_local), bf16),
-                pltpu.VMEM((1, tok_rows), f32),
+                pltpu.VMEM((tp, 1, tok_rows), f32),
                 pltpu.VMEM((1, d_local), f32),
             ],
             in_specs=[hbm] * 4,
@@ -280,16 +288,13 @@
                 pltpu.VMEM((2 * blocks, ROWS, d_local // 2), f32),
                 pltpu.VMEM((2 * blocks, ROWS, d_local // 2), f32),
                 pltpu.VMEM((tok_rows, d_local), bf16),
-                pltpu.VMEM((tp, 1, tok_rows), f32),
                 dma((2,)),
                 dma((W_SLOTS,)),
                 dma,
                 dma,
                 dma,
                 dma,
-                dma,
-                dma,
-                dma((2 * blocks,)),
+                dma((3,)),
                 dma((2,)),
             ],
             compiler_params=pltpu.CompilerParams(

time: 79.2 us -> 79.1 us (level)
  no operation moved by 1% of the time
where the time goes in v8:
time: 79.1 us; the launch traced here: 79 us
  Pallas kernels  78.3 us (99%)
    pallas_call x1, Pallas kernels, local_step(): pl.pallas_call(functools.partial(reduce_kernel, tp, d_local), out_shape=[...  77 us

profile of v8, /device:TPU:81, one launch (start us, length us, event | category | flops | bytes accessed | tf_op | source)
XLA Modules:
  0.0 79.0 jit_solution(7493646921600487415)
XLA Ops:
  0.6 77.0 %project_reduce.1 = (f32[256,2048]{1,0:T(8,128)S(1)}, bf16[256,2048]{1,0:T(8,128)(2,1)S(1)}, f32[8,1,256]{2,1,0:T(1,128)S(1)}, f32[1,2048]{1,0:T(1,128)S(1)}) custom-call(bf16[256,2048]{1,0:T(8,128)(2,1)} %a_hbm.1, bf16[2048,16384]{1,0:T(8,128)(2,1)} %w_hbm.1, bf16[256,2048]{1,0:T(8,128)(2,1)} %r_hbm.1, f32[1,2048]{1,0:T(1,128)} %bitcast.1), custom_call_target="tpu_custom_call" | custom-call | tf_op jit(solution)/shard_map/project_reduce/pallas_call | solution.py:273
  77.6 1.3 %norm_write.1 = (bf16[256,2048]{1,0:T(8,128)(2,1)}, bf16[256,2048]{1,0:T(8,128)(2,1)}) custom-call(f32[256,2048]{1,0:T(8,128)S(1)} %get-tuple-element.6.hid, bf16[256,2048]{1,0:T(8,128)(2,1)S(1)} %get-tuple-element.7.hid_bf, f32[8,1,256]{2,1,0:T(1,128)S(1)} %get-tuple-element.8.sq_all, f32[1,2048]{1,0:T(1,128)S(1)} %get-tuple-element.9.gain), custom_call_target="tpu_custom_call" | custom-call | tf_op jit(solution)/shard_map/norm_write/pallas_call | solution.py:305

commit v9 on v8

--- a/solution.py
+++ b/solution.py
@@ -88,7 +88,7 @@
         return [((chip + hop) % chips) * CORES + b for hop in hops for b in range(CORES)]
 
     partner = chip * CORES + 1 - core
-    others = sorted(range(1, chips), key=lambda hop: -min(hop, chips - hop))
+    others = sorted(range(1, chips), key=lambda hop: min(hop, chips - hop))
 
     def sq_copy(peer):
         return pltpu.make_async_remote_copy(
@@ -222,8 +222,8 @@
                 by_lane, axis=0, keepdims=True
             )
             totals = []
-    far_first = peers(others)
-    for peer in far_first[1::CORES] + [partner] + far_first[::CORES]:
+    near_first = peers(others)
+    for peer in near_first[1::CORES] + [partner] + near_first[::CORES]:
         sq_copy(peer).start()
 
     def narrow(rb, carry):

time: 79.1 us -> 79.1 us (level)
  no operation moved by 1% of the time
where the time goes in v9:
time: 79.1 us; the launch traced here: 79 us
  Pallas kernels  78.4 us (99%)
    pallas_call x1, Pallas kernels, local_step(): pl.pallas_call(functools.partial(reduce_kernel, tp, d_local), out_shape=[...  77 us

profile of v9, /device:TPU:81, one launch (start us, length us, event | category | flops | bytes accessed | tf_op | source)
XLA Modules:
  0.0 79.0 jit_solution(10919692954617750209)
XLA Ops:
  0.6 77.0 %project_reduce.1 = (f32[256,2048]{1,0:T(8,128)S(1)}, bf16[256,2048]{1,0:T(8,128)(2,1)S(1)}, f32[8,1,256]{2,1,0:T(1,128)S(1)}, f32[1,2048]{1,0:T(1,128)S(1)}) custom-call(bf16[256,2048]{1,0:T(8,128)(2,1)} %a_hbm.1, bf16[2048,16384]{1,0:T(8,128)(2,1)} %w_hbm.1, bf16[256,2048]{1,0:T(8,128)(2,1)} %r_hbm.1, f32[1,2048]{1,0:T(1,128)} %bitcast.1), custom_call_target="tpu_custom_call" | custom-call | tf_op jit(solution)/shard_map/project_reduce/pallas_call | solution.py:273
  77.7 1.3 %norm_write.1 = (bf16[256,2048]{1,0:T(8,128)(2,1)}, bf16[256,2048]{1,0:T(8,128)(2,1)}) custom-call(f32[256,2048]{1,0:T(8,128)S(1)} %get-tuple-element.6.hid, bf16[256,2048]{1,0:T(8,128)(2,1)S(1)} %get-tuple-element.7.hid_bf, f32[8,1,256]{2,1,0:T(1,128)S(1)} %get-tuple-element.8.sq_all, f32[1,2048]{1,0:T(1,128)S(1)} %get-tuple-element.9.gain), custom_call_target="tpu_custom_call" | custom-call | tf_op jit(solution)/shard_map/norm_write/pallas_call | solution.py:305

commit v10 on v8

--- a/solution.py
+++ b/solution.py
@@ -101,16 +101,24 @@
         )
 
     top, low = slice(0, tok_rows // 2), slice(tok_rows // 2, tok_rows)
-    a_copies = [
-        pltpu.make_async_copy(a_hbm.at[rows], a.at[rows], a_sem.at[i])
-        for i, rows in enumerate((top, low))
-    ]
+    deep = a.shape[1] // 2
+    first = []
+    for k, a_half_sem, w_half_sem in ((0, a_sem.at[0], w_sem.at[0]), (deep, rsend_sem, q_sem.at[0])):
+        ks, cols = pl.ds(k, deep), pl.ds(pl.multiple_of(w_col(0), COLS), COLS)
+        first.append(
+            (
+                pltpu.make_async_copy(a_hbm.at[top, ks], a.at[top, ks], a_half_sem),
+                pltpu.make_async_copy(w_hbm.at[ks, cols], w.at[0, ks], w_half_sem),
+            )
+        )
+    a_low = pltpu.make_async_copy(a_hbm.at[low], a.at[low], a_sem.at[1])
     r_copy = pltpu.make_async_copy(r_hbm, res, a_sem.at[0])
     g_copy = pltpu.make_async_copy(g_hbm, gain, a_sem.at[1])
-    a_copies[0].start()
-    w_copy(0).start()
+    for copies in first:
+        for copy in copies:
+            copy.start()
     w_copy(1).start()
-    a_copies[1].start()
+    a_low.start()
     barrier = pltpu.get_barrier_semaphore()
     near = peers((1, chips - 1)) + [partner]
     for peer in near:
@@ -125,15 +133,21 @@
             a[rows], w[g % W_SLOTS], preferred_element_type=jnp.float32
         ).astype(jnp.bfloat16)
 
-    for i, rows in enumerate((top, low)):
-        a_copies[i].wait()
-        for g in range(2):
-            if i == 0:
-                w_copy(g).wait()
-            project(g, rows)
-            if i == 0 and g == 0:
-                pl.semaphore_wait(barrier, len(near))
-            piece_copy(g, mid_sem, rows).start()
+    total = jnp.zeros((tok_rows // 2, COLS), jnp.float32)
+    for copies, ks in zip(first, (slice(0, deep), slice(deep, 2 * deep))):
+        for copy in copies:
+            copy.wait()
+        total += jnp.dot(a[top, ks], w[0, ks], preferred_element_type=jnp.float32)
+    part[0, top] = total.astype(jnp.bfloat16)
+    pl.semaphore_wait(barrier, len(near))
+    piece_copy(0, mid_sem, top).start()
+    w_copy(1).wait()
+    project(1, top)
+    piece_copy(1, mid_sem, top).start()
+    a_low.wait()
+    for g in range(2):
+        project(g, low)
+        piece_copy(g, mid_sem, low).start()
     for g in range(2):
         w_copy(W_SLOTS + g).start()
 

time: 79.1 us -> 79.1 us (level)
  no operation moved by 1% of the time
where the time goes in v10:
time: 79.1 us; the launch traced here: 79 us
  Pallas kernels  78.3 us (99%)
    pallas_call x1, Pallas kernels, local_step(): pl.pallas_call(functools.partial(reduce_kernel, tp, d_local), out_shape=[...  77 us

profile of v10, /device:TPU:81, one launch (start us, length us, event | category | flops | bytes accessed | tf_op | source)
XLA Modules:
  0.0 79.0 jit_solution(12447195830043514953)
XLA Ops:
  0.6 77.0 %project_reduce.1 = (f32[256,2048]{1,0:T(8,128)S(1)}, bf16[256,2048]{1,0:T(8,128)(2,1)S(1)}, f32[8,1,256]{2,1,0:T(1,128)S(1)}, f32[1,2048]{1,0:T(1,128)S(1)}) custom-call(bf16[256,2048]{1,0:T(8,128)(2,1)} %a_hbm.1, bf16[2048,16384]{1,0:T(8,128)(2,1)} %w_hbm.1, bf16[256,2048]{1,0:T(8,128)(2,1)} %r_hbm.1, f32[1,2048]{1,0:T(1,128)} %bitcast.1), custom_call_target="tpu_custom_call" | custom-call | tf_op jit(solution)/shard_map/project_reduce/pallas_call | solution.py:287
  77.6 1.3 %norm_write.1 = (bf16[256,2048]{1,0:T(8,128)(2,1)}, bf16[256,2048]{1,0:T(8,128)(2,1)}) custom-call(f32[256,2048]{1,0:T(8,128)S(1)} %get-tuple-element.6.hid, bf16[256,2048]{1,0:T(8,128)(2,1)S(1)} %get-tuple-element.7.hid_bf, f32[8,1,256]{2,1,0:T(1,128)S(1)} %get-tuple-element.8.sq_all, f32[1,2048]{1,0:T(1,128)S(1)} %get-tuple-element.9.gain), custom_call_target="tpu_custom_call" | custom-call | tf_op jit(solution)/shard_map/norm_write/pallas_call | solution.py:319

commit v11 on v10

--- a/solution.py
+++ b/solution.py
@@ -11,7 +11,7 @@
 CORES = 2
 COLS = 256
 W_SLOTS = 4
-ROWS = 64
+ROWS = 32
 OUT_ROWS = 128
 
 

time: 79.1 us -> 79.1 us (level)
  no operation moved by 1% of the time
where the time goes in v11:
time: 79.1 us; the launch traced here: 78.9 us
  Pallas kernels  78.3 us (99%)
    pallas_call x1, Pallas kernels, local_step(): pl.pallas_call(functools.partial(reduce_kernel, tp, d_local), out_shape=[...  77 us

profile of v11, /device:TPU:81, one launch (start us, length us, event | category | flops | bytes accessed | tf_op | source)
XLA Modules:
  0.0 78.9 jit_solution(11951018121728116468)
XLA Ops:
  0.6 77.0 %project_reduce.1 = (f32[256,2048]{1,0:T(8,128)S(1)}, bf16[256,2048]{1,0:T(8,128)(2,1)S(1)}, f32[8,1,256]{2,1,0:T(1,128)S(1)}, f32[1,2048]{1,0:T(1,128)S(1)}) custom-call(bf16[256,2048]{1,0:T(8,128)(2,1)} %a_hbm.1, bf16[2048,16384]{1,0:T(8,128)(2,1)} %w_hbm.1, bf16[256,2048]{1,0:T(8,128)(2,1)} %r_hbm.1, f32[1,2048]{1,0:T(1,128)} %bitcast.1), custom_call_target="tpu_custom_call" | custom-call | tf_op jit(solution)/shard_map/project_reduce/pallas_call | solution.py:287
  77.6 1.3 %norm_write.1 = (bf16[256,2048]{1,0:T(8,128)(2,1)}, bf16[256,2048]{1,0:T(8,128)(2,1)}) custom-call(f32[256,2048]{1,0:T(8,128)S(1)} %get-tuple-element.6.hid, bf16[256,2048]{1,0:T(8,128)(2,1)S(1)} %get-tuple-element.7.hid_bf, f32[8,1,256]{2,1,0:T(1,128)S(1)} %get-tuple-element.8.sq_all, f32[1,2048]{1,0:T(1,128)S(1)} %get-tuple-element.9.gain), custom_call_target="tpu_custom_call" | custom-call | tf_op jit(solution)/shard_map/norm_write/pallas_call | solution.py:319
